TPU v7x, 32 devices: a whole 2x2x4 slice. The times are simulated.
32 devices in a mesh: tm: 8 (over z, y), freq: 4 (over x, core).
Axes of the slice: x: 2, y: 2, z: 4, core: 2. Of those that a mesh axis runs over, the one named last changes fastest.
Arguments:
- snapshots: bfloat16 [4352, 3, 4096], P('tm', None, 'freq'), may hold values from -200 to 200
- block_starts: int32 [32], replicated, may hold values from 0 to 4032, as said below
- freq_index: int32 [16], replicated, may hold values from 0 to 128
Outputs:
- modes: bfloat16 [16, 32, 2, 3, 4096], P(None, None, None, None, ('freq', 'tm'))
- energy: float32 [16], replicated
Inputs may be any that keep to these rules, and one draw needn't show every extreme that they name: `block_starts`: block b starts at b * 128 plus between 0 and 64.
All inputs are finite; a program needn't handle non-finite values.
Results may differ from a plain program's by a relative error of at most 0.0085.
Values may be sent and summed in bfloat16 or wider, within the bound.
A program may use at most 64 MiB of HBM per device.

v0:
```python
import math

import jax
import jax.numpy as jnp
from jax import lax
from jax.sharding import PartitionSpec as P

NB = 32
NFFT = 256
NF = 16
NSIT = 6


def for_sending(shard):
    return jax.tree.map(lambda a: a.astype(jnp.bfloat16) if a.dtype == jnp.float32 else a, shard)


def dft_rows(freq_index):
    times_idx = jnp.arange(NFFT, dtype=jnp.int32)
    phase_int = freq_index[:, None] * times_idx[None, :] % NFFT
    angles = 2.0 * math.pi / NFFT * phase_int.astype(jnp.float32)
    window = 0.5 - 0.5 * jnp.cos(2.0 * math.pi / NFFT * times_idx.astype(jnp.float32))
    scaling = 1.0 / jnp.sqrt(jnp.sum(window * window))
    cosine = window[None, :] * jnp.cos(angles) * scaling
    sine_rows = -window[None, :] * jnp.sin(angles) * scaling
    return jnp.stack([cosine, sine_rows], 1).reshape(2 * NF, NFFT).astype(jnp.bfloat16)


def block_rows(block_starts):
    return block_starts[:, None] + jnp.arange(NFFT, dtype=jnp.int32)[None, :]


def matmul_batch(left, right):
    return jnp.einsum("fij,fjk->fik", left, right, precision=lax.Precision.HIGHEST)


def whiten(summed, points):
    gram_re = summed[:, 0]
    gram_im = summed[:, 1]
    top_rows = jnp.concatenate([gram_re, -gram_im], 2)
    low_rows = jnp.concatenate([gram_im, gram_re], 2)
    hermit = jnp.concatenate([top_rows, low_rows], 1)
    frob = jnp.sqrt(jnp.sum(hermit * hermit, axis=(1, 2)) + 1e-06)
    identity = jnp.eye(2 * NB, dtype=jnp.float32)[None]
    iterate = hermit / frob[:, None, None]
    inverse = jnp.broadcast_to(identity, hermit.shape)
    for iteration in range(NSIT):
        factor = 1.5 * identity - 0.5 * matmul_batch(inverse, iterate)
        iterate = matmul_batch(iterate, factor)
        inverse = matmul_batch(factor, inverse)
    columns = inverse[:, :, :NB] * jnp.sqrt(6.0 * points / frob)[:, None, None]
    upper = columns[:, :NB]
    lower = columns[:, NB:]
    coefficients = jnp.stack([jnp.stack([upper, -lower], 1), jnp.stack([lower, upper], 1)], 1)
    energy = jnp.trace(gram_re, axis1=1, axis2=2) / (3.0 * NB * points)
    return (coefficients, energy)


def local(snapshots, block_starts, freq_index):
    dft_table = dft_rows(freq_index)
    offsets = block_rows(block_starts)
    series = lax.all_to_all(snapshots, "tm", split_axis=2, concat_axis=0, tiled=True)
    count = series.shape[1]
    width = series.shape[2]
    columns_all = series.reshape(series.shape[0], count * width)
    windows = jnp.take(columns_all, offsets, axis=0)
    spectra_part = jnp.einsum(
        "rt,btn->rbn", dft_table, windows, preferred_element_type=jnp.float32
    ).astype(jnp.bfloat16)
    spectra = spectra_part.reshape(2 * NF, NB, count, width)
    width = spectra.shape[3]
    points = float(width * lax.axis_size("tm") * lax.axis_size("freq"))
    flat_spec = spectra.reshape(NF, 2, NB, 3 * width)
    real_part = flat_spec[:, 0]
    imag_part = flat_spec[:, 1]
    gram_re = jnp.einsum("fbn,fcn->fbc", real_part, real_part, preferred_element_type=jnp.float32)
    gram_re = gram_re + jnp.einsum(
        "fbn,fcn->fbc", imag_part, imag_part, preferred_element_type=jnp.float32
    )
    cross_terms = jnp.einsum(
        "fbn,fcn->fbc", real_part, imag_part, preferred_element_type=jnp.float32
    )
    partial_gram = jnp.stack([gram_re, cross_terms - jnp.swapaxes(cross_terms, 1, 2)], 1)
    shared = lax.psum_scatter(partial_gram, "freq", scatter_dimension=0, tiled=True)
    shared = lax.psum(shared, "tm")
    coef_part, energy_part = whiten(shared, points)
    coefficients, energy = (
        lax.all_gather(for_sending(coef_part), "freq", axis=0, tiled=True).astype(coef_part.dtype),
        lax.all_gather(for_sending(energy_part), "freq", axis=0, tiled=True).astype(
            energy_part.dtype
        ),
    )
    coef_bf = jnp.transpose(coefficients.astype(jnp.bfloat16), (0, 4, 1, 2, 3))
    modes = jnp.einsum(
        "fjorb,frbn->fjon", coef_bf, flat_spec, preferred_element_type=jnp.float32
    ).astype(jnp.bfloat16)
    return (modes.reshape(NF, NB, 2, 3, width), energy)


def solution(mesh):
    return jax.shard_map(
        local,
        mesh=mesh,
        in_specs=(P("tm", None, "freq"), P(), P()),
        out_specs=(P(None, None, None, None, ("freq", "tm")), P()),
        check_vma=False,
    )
```

profile of v0, /device:TPU:0, one launch (start us, length us, event | category | flops | bytes accessed | tf_op | source)
XLA Modules:
  0.0 302.0 jit_solution(5454978820925684729)
XLA Ops:
  7.2 8.6 %copy.43 = bf16[544,3,1024]{0,1,2:T(4,128)(2,1)} copy(bf16[544,3,1024]{2,0,1:T(8,128)(2,1)} %param.3) | data formatting | bytes 6684672 | tf_op args[0]
  15.8 7.4 %all-to-all-start = ((bf16[544,3,1024]{0,1,2:T(4,128)(2,1)}), bf16[544,3,1024]{0,1,2:T(4,128)(2,1)}, u32[]{:S(2)}, u32[]{:S(2)}) async-start(bf16[544,3,1024]{0,1,2:T(4,128)(2,1)} %copy.43), calls=%async_computation | async-start | bytes 10485760 | tf_op jit(solution)/shard_map/all_to_all | solution.py:62
  23.3 0.6 multiply_reduce_fusion.1
  25.0 0.6 fusion.43
  27.1 111.9 %all-to-all-done = bf16[544,3,1024]{0,1,2:T(4,128)(2,1)} async-done(((bf16[544,3,1024]{0,1,2:T(4,128)(2,1)}), bf16[544,3,1024]{0,1,2:T(4,128)(2,1)}, u32[]{:S(2)}, u32[]{:S(2)}) %all-to-all-start) | async-done | bytes 3342368 | tf_op jit(solution)/shard_map/all_to_all | solution.py:62
  139.0 7.4 %copy.74 = bf16[544,3,8,128]{0,2,3,1:T(8,128)(2,1)} copy(bf16[544,3,8,128]{0,1,3,2:T(4,128)(2,1)} %bitcast) | data formatting | bytes 6684672 | tf_op jit(solution)/shard_map/all_to_all | solution.py:62
  146.4 7.4 %reshape.243 = bf16[4352,384]{0,1:T(8,128)(2,1)} reshape(bf16[8,544,3,128]{1,0,3,2:T(8,128)(2,1)} %bitcast.97) | data formatting | bytes 6684672 | tf_op jit(solution)/shard_map/reshape | solution.py:65
  153.7 5.6 %copy.45 = bf16[4352,384]{1,0:T(8,128)(2,1)S(1)} copy(bf16[4352,384]{0,1:T(8,128)(2,1)} %reshape.243) | data formatting | bytes 6684672 | tf_op jit(solution)/shard_map/reshape | solution.py:65
  159.4 33.1 %gather_fusion = bf16[8192,384]{1,0:T(8,128)(2,1)} fusion(bf16[4352,384]{1,0:T(8,128)(2,1)S(1)} %copy.45, s32[8192]{0:T(1024)S(1)} %broadcast_clamp_fusion), kind=kCustom, calls=%fused_computation | custom fusion | bytes 12615680 | tf_op jit(solution)/shard_map/jit(_take)/gather | solution.py:66
  192.5 4.6 %fusion.4 = bf16[32,32,384]{2,0,1:T(8,128)(2,1)S(1)} fusion(bf16[32,256,1]{1,0,2:T(8,128)(2,1)S(1)} %reshape.260, bf16[32,256,384]{2,1,0:T(8,128)(2,1)} %bitcast.99, pred[32,256]{1,0:T(8,128)(4,1)S(1)} %fusion.31), kind=kOutput, calls=%fused_computation.7 | convolution fusion | flops 204865536 | bytes 7102464 | tf_op jit(solution)/shard_map/rt,btn->rbn/dot_general | solution.py:67
  197.1 0.3 reshape_reshape.3
  197.4 1.1 fusion.42
  198.5 0.3 fusion.18
  198.8 0.5 fusion.17
  199.6 0.3 fusion.7
  199.9 0.8 pad_maximum_fusion
  200.8 32.6 %all-reduce.4.cloned.1.call-done = f32[16,2,32,32]{3,2,0,1:T(8,128)} async-done(((f32[16,2,32,32]{3,2,0,1:T(8,128)}), f32[16,2,32,32]{3,2,0,1:T(8,128)}) %all-reduce.4.cloned.1.call-update) | async-done | bytes 131088
  233.4 0.9 constant_dynamic-slice_fusion
  234.3 38.6 %psum.7 = f32[4,2,32,32]{3,2,0,1:T(8,128)S(1)} all-reduce(f32[4,2,32,32]{3,2,0,1:T(8,128)S(1)} %constant_dynamic-slice_fusion), channel_id=1, replica_groups=mesh['tm'=8,'freq'=4] {'tm'}, use_global_device_ids=true, to_apply=%region_2.3 | all-reduce | flops 8192 | bytes 65536 | tf_op jit(solution)/shard_map/psum | solution.py:85
  273.3 0.4 fusion.13
  273.7 0.3 fusion.41
  274.2 0.3 fusion.12
  275.0 0.3 fusion.11
  275.8 0.3 fusion.10
  277.4 0.3 fusion.8
  277.7 0.4 convolution_multiply_fusion.6
  278.3 6.5 %all_gather.6 = bf16[16,2,2,32,32]{3,4,0,2,1:T(8,128)(2,1)S(1)} all-gather(bf16[4,2,2,32,32]{3,4,0,2,1:T(8,128)(2,1)S(1)} %pad_maximum_fusion.1), channel_id=1, replica_groups=mesh['tm'=8,'freq'=4] {'freq'}, dimensions={0}, use_global_device_ids=true | all-gather | bytes 163840 | tf_op jit(solution)/shard_map/all_gather | solution.py:88
  284.8 0.4 bitcast_convert_fusion
  285.2 0.3 reshape.244
  285.8 2.1 copy.52
  287.9 6.8 %all-reduce = bf16[16]{0:T(256)(128)(2,1)S(1)} all-reduce(bf16[16]{0:T(256)(128)(2,1)S(1)} %dynamic-update-slice), channel_id=1, replica_groups=mesh['tm'=8,'freq'=4] {'freq'}, use_global_device_ids=true, to_apply=%add | all-reduce | flops 16 | bytes 64
  294.7 0.5 convert_element_type.64
  (43 shorter events, 4.1 us)
Async XLA Ops:
  15.8 8.9 %copy-start.2 = (s32[16]{0:T(128)S(1)}, s32[16]{0:T(128)}, u32[]{:S(2)}) copy-start(s32[16]{0:T(128)} %param.5) | copy-start | bytes 196
  15.8 9.1 %copy-start = (s32[32]{0:T(128)S(1)}, s32[32]{0:T(128)}, u32[]{:S(2)}) copy-start(s32[32]{0:T(128)} %param.4) | copy-start | bytes 388
  15.8 9.2 %copy-start.1 = (u32[32]{0:T(128)S(1)}, u32[32]{0:T(128)}, u32[]{:S(2)}) copy-start(u32[32]{0:T(128)} %constant.55) | copy-start | bytes 388
  15.8 123.2 %all-to-all-start = ((bf16[544,3,1024]{0,1,2:T(4,128)(2,1)}), bf16[544,3,1024]{0,1,2:T(4,128)(2,1)}, u32[]{:S(2)}, u32[]{:S(2)}) async-start(bf16[544,3,1024]{0,1,2:T(4,128)(2,1)} %copy.43), calls=%async_computation | async-start | bytes 10485760 | tf_op jit(solution)/shard_map/all_to_all | solution.py:62
  23.2 210.1 %all-reduce.4.cloned.1.call-start = ((), (), s32[]{:S(2)}) async-start(), calls=%async_computation.1 | async-start | bytes 1048576
Sparse Core Ops, SparseCore 0:
  200.9 32.4 all-reduce.3
where the time goes:
time: 303 us; the launch traced here: 302 us
  waiting for transfers between devices  145 us (48%)
  local copies, waits for them, and re-layouts  67.9 us (22%)
  blocking collectives  51.9 us (17%)
  between operations  16.4 us (5%)
  matrix products  10.8 us (4%)
  starting transfers between devices  7.49 us (2%)
    all_to_all x1, waiting for transfers between devices, local(): lax.all_to_all(snapshots, 'tm', split_axis=2, concat_axis=0, tiled=True)  112 us
    psum x1, blocking collectives, local(): shared = lax.psum(shared, 'tm')  38.6 us
    gather x1, local copies, waits for them, and re-layouts, local(): windows = jnp.take(columns_all, offsets, axis=0)  33.1 us
    unnamed x2, waiting for transfers between devices  32.6 us
    reshape x2, local copies, waits for them, and re-layouts, local(): columns_all = series.reshape(series.shape[0], count * width)  13 us
    unnamed x13, local copies, waits for them, and re-layouts  12.5 us
    all_to_all x1, starting transfers between devices, local(): lax.all_to_all(snapshots, 'tm', split_axis=2, concat_axis=0, tiled=True)  7.45 us
    all_to_all x1, local copies, waits for them, and re-layouts, local(): lax.all_to_all(snapshots, 'tm', split_axis=2, concat_axis=0, tiled=True)  7.37 us
  transfers between devices with their start and end apart: 2, of which 2 were waited for; matrix products, arithmetic and copies ran while one was open for 1% of the time, Pallas kernels for 0%

commit v1 on v0

--- a/solution.py
+++ b/solution.py
@@ -1,8 +1,11 @@
+import functools
 import math
 
 import jax
 import jax.numpy as jnp
 from jax import lax
+from jax.experimental import pallas as pl
+from jax.experimental.pallas import tpu as pltpu
 from jax.sharding import PartitionSpec as P
 
 NB = 32
@@ -97,9 +100,346 @@
     return (modes.reshape(NF, NB, 2, 3, width), energy)
 
 
+MESH = pl.DeviceIdType.MESH
+ROWS = 2 * NF
+HOP = 128
+JIT = 64
+
+
+def plan(n, rows, total, width):
+    if n < 2 or NB % n or total % NF or total // NF < 1 or width != 128 or rows % 16:
+        return None
+    per = NB // n
+    if per < 4:
+        return None
+    left, right = [[], []], [[], []]
+    for dev in range(n):
+        first, end = rows * dev, rows * (dev + 1)
+        for block in range(NB):
+            if HOP * block >= end or HOP * block + JIT + NFFT <= first:
+                continue
+            owner = block // per
+            if owner == dev:
+                continue
+            if owner == dev - 1 and per * dev - block <= 2:
+                left[per * dev - block - 1].append(dev)
+            elif owner == dev + 1 and block - per * (dev + 1) < 2:
+                right[block - per * (dev + 1)].append(dev)
+            else:
+                return None
+    for devs in left + right:
+        if devs and devs != list(range(devs[0], devs[-1] + 1)):
+            return None
+    return per, left, right
+
+
+def shifted_tables(block_starts, freq_index, n, per, rows):
+    me = lax.axis_index("tm")
+    offsets = jnp.array([-1, -2, per, per + 1] + list(range(per)), dtype=jnp.int32)
+    ids = per * me + offsets
+    starts = jnp.take(block_starts, jnp.clip(ids, 0, NB - 1))
+    local_t = rows * me + jnp.arange(rows, dtype=jnp.int32)[None, :] - starts[:, None]
+    inside = (local_t >= 0) & (local_t < NFFT) & ((ids >= 0) & (ids < NB))[:, None]
+    local_t = jnp.where(inside, local_t, 0)
+    times_idx = jnp.arange(NFFT, dtype=jnp.int32)
+    full_window = 0.5 - 0.5 * jnp.cos(2.0 * math.pi / NFFT * times_idx.astype(jnp.float32))
+    scaling = 1.0 / jnp.sqrt(jnp.sum(full_window * full_window))
+    window = 0.5 - 0.5 * jnp.cos(2.0 * math.pi / NFFT * local_t.astype(jnp.float32))
+    window = jnp.where(inside, window, 0.0)
+    freqs = jnp.repeat(freq_index, 2)
+    phase = freqs[None, :, None] * local_t[:, None, :] % NFFT
+    angles = 2.0 * math.pi / NFFT * phase.astype(jnp.float32)
+    is_sine = (jnp.arange(ROWS) % 2 == 1)[None, :, None]
+    wave = jnp.where(is_sine, -jnp.sin(angles), jnp.cos(angles))
+    table = window[:, None, :] * wave * scaling
+    return table.reshape((per + 4) * ROWS, rows).astype(jnp.bfloat16)
+
+
+def expanders():
+    row = jnp.arange(NB * 6)
+    col = jnp.arange(2 * NB)
+    spread = (row[:, None] // 6 == col[None, :] % NB) & (row[:, None] % 2 == col[None, :] // NB)
+    wide = jnp.arange(3 * 2 * NB)
+    mask = row[:, None] // 2 % 3 == wide[None, :] // (2 * NB)
+    return spread.astype(jnp.bfloat16), mask.astype(jnp.float32)
+
+
+def within(me, devs):
+    return (me >= devs[0]) & (me <= devs[-1])
+
+
+def kernel(n, nf_dev, per, left, right, points, x_hbm, t_ref, spread_ref, mask_ref,
+           modes_ref, energy_ref, xv, out_l, out_r, in_l, in_r, own, sendb, recvb, spec32, spec,
+           gpart, gath, msg, crecv, load_sem, lsend, lrecv, rsend, rrecv, asend, arecv,
+           gsend, grecv, csend, crcv):
+    tm = lax.axis_index("tm")
+    fr = lax.axis_index("freq")
+    total = n * nf_dev
+    lin = tm * nf_dev + fr
+    stride = total // NF
+
+    def where_is(index):
+        return {"tm": index // nf_dev, "freq": index % nf_dev}
+
+    for c in range(3):
+        pltpu.make_async_copy(x_hbm.at[c], xv.at[c], load_sem.at[c]).start()
+    barrier = pltpu.get_barrier_semaphore()
+
+    @pl.loop(1, total)
+    def _(k):
+        pl.semaphore_signal(barrier, inc=1, device_id=where_is((lin + k) % total), device_id_type=MESH)
+
+    width = xv.shape[2]
+    for c in range(3):
+        pltpu.make_async_copy(x_hbm.at[c], xv.at[c], load_sem.at[c]).wait()
+        part = jnp.dot(t_ref[: 4 * ROWS, :], xv[c], preferred_element_type=jnp.float32)
+        for slot in range(2):
+            out_l[slot, :, c * width : (c + 1) * width] = part[slot * ROWS : (slot + 1) * ROWS]
+            out_r[slot, :, c * width : (c + 1) * width] = part[(slot + 2) * ROWS : (slot + 3) * ROWS]
+    pl.semaphore_wait(barrier, total - 1)
+
+    def to_left(slot):
+        return pltpu.make_async_remote_copy(
+            src_ref=out_l.at[slot], dst_ref=in_r.at[slot], send_sem=lsend.at[slot],
+            recv_sem=lrecv.at[slot], device_id={"tm": (tm + n - 1) % n, "freq": fr},
+            device_id_type=MESH)
+
+    def to_right(slot):
+        return pltpu.make_async_remote_copy(
+            src_ref=out_r.at[slot], dst_ref=in_l.at[slot], send_sem=rsend.at[slot],
+            recv_sem=rrecv.at[slot], device_id={"tm": (tm + 1) % n, "freq": fr},
+            device_id_type=MESH)
+
+    for slot in range(2):
+        for devs, make in ((left[slot], to_left), (right[slot], to_right)):
+            if devs:
+                @pl.when(within(tm, devs))
+                def _(make=make, slot=slot):
+                    make(slot).start()
+
+    for c in range(3):
+        own[:, c * width : (c + 1) * width] = jnp.dot(
+            t_ref[4 * ROWS :, :], xv[c], preferred_element_type=jnp.float32)
+
+    def scatter(block, k):
+        dest = (tm + k) % n
+        return pltpu.make_async_remote_copy(
+            src_ref=sendb.at[dest, block], dst_ref=recvb.at[tm, block],
+            send_sem=asend.at[block, dest], recv_sem=arecv.at[block, tm],
+            device_id={"tm": dest, "freq": fr}, device_id_type=MESH)
+
+    order = list(range(2, per - 2)) + [1, per - 2, per - 1, 0]
+    for block in order:
+        span = slice(block * ROWS, (block + 1) * ROWS)
+        if block < 2 and right[block]:
+            @pl.when(within(tm - 1, right[block]))
+            def _(block=block, span=span):
+                to_right(block).wait_recv()
+                own[span, :] += in_l[block]
+        back = per - 1 - block
+        if back < 2 and left[back]:
+            @pl.when(within(tm + 1, left[back]))
+            def _(back=back, span=span):
+                to_left(back).wait_recv()
+                own[span, :] += in_r[back]
+        pw = width // n
+        for dest in range(n):
+            for c in range(3):
+                sendb[dest, block, :, c * pw : (c + 1) * pw] = own[
+                    span, c * width + dest * pw : c * width + (dest + 1) * pw].astype(jnp.bfloat16)
+
+        @pl.loop(1, n)
+        def _(k, block=block):
+            scatter(block, k).start()
+
+    def widen(src, block, values):
+        base = (src * per + block) * ROWS
+        for c in range(3):
+            spec32[c, pl.ds(pl.multiple_of(base, ROWS), ROWS), :] = values[:, c * 128 : (c + 1) * 128].astype(jnp.float32)
+
+    for block in range(per):
+        widen(tm, block, sendb[tm, block])
+
+    @pl.loop(1, n)
+    def _(k):
+        src = (tm + n - k) % n
+        for block in range(per):
+            pltpu.make_async_remote_copy(
+                src_ref=sendb.at[src, block], dst_ref=recvb.at[src, block],
+                send_sem=asend.at[block, src], recv_sem=arecv.at[block, src],
+                device_id={"tm": src, "freq": fr}, device_id_type=MESH).wait_recv()
+            widen(src, block, recvb[src, block])
+
+    def to_owner(f):
+        return pltpu.make_async_remote_copy(
+            src_ref=gpart.at[f], dst_ref=gath.at[lin], send_sem=gsend.at[f],
+            recv_sem=grecv.at[lin], device_id=where_is(f * stride), device_id_type=MESH)
+
+    for f in range(NF):
+        real = [spec32[c, pl.ds(2 * f, NB, stride=ROWS), :].astype(jnp.bfloat16) for c in range(3)]
+        imag = [spec32[c, pl.ds(2 * f + 1, NB, stride=ROWS), :].astype(jnp.bfloat16) for c in range(3)]
+        for c in range(3):
+            spec[f, c * 2 * NB : c * 2 * NB + NB, :] = real[c]
+            spec[f, c * 2 * NB + NB : (c + 1) * 2 * NB, :] = imag[c]
+        lhs = jnp.concatenate(real + imag, axis=1)
+        rhs = jnp.concatenate([lhs, jnp.concatenate(imag + [-v for v in real], axis=1)], axis=0)
+        gram = lax.dot_general(lhs, rhs, (((1,), (1,)), ((), ())), preferred_element_type=jnp.float32)
+        half = NB // 2
+        gpart[f] = jnp.concatenate([gram[:half], gram[half:]], axis=1)
+
+        @pl.when(lin != f * stride)
+        def _(f=f):
+            to_owner(f).start()
+
+    def coef_to(index):
+        return pltpu.make_async_remote_copy(
+            src_ref=msg, dst_ref=crecv.at[lin // stride], send_sem=csend.at[index],
+            recv_sem=crcv.at[lin // stride], device_id=where_is(index), device_id_type=MESH)
+
+    @pl.when(lin % stride == 0)
+    def _():
+        f_mine = lin // stride
+        gath[lin] = gpart[f_mine]
+
+        @pl.loop(1, total)
+        def _(k):
+            src = (lin + k) % total
+            pltpu.make_async_remote_copy(
+                src_ref=gpart.at[0], dst_ref=gath.at[src], send_sem=gsend.at[0],
+                recv_sem=grecv.at[src], device_id=where_is(src), device_id_type=MESH).wait_recv()
+
+        packed = jnp.sum(gath[...], axis=0)
+        both = jnp.concatenate([packed[:, : 2 * NB], packed[:, 2 * NB :]], axis=0)
+        gram_re = both[:, :NB]
+        gram_im = both[:, NB:]
+        hermit = jnp.concatenate([
+            jnp.concatenate([gram_re, -gram_im], axis=1),
+            jnp.concatenate([gram_im, gram_re], axis=1)], axis=0)
+        frob = jnp.sqrt(jnp.sum(hermit * hermit, axis=(0, 1), keepdims=True) + 1e-06)
+        ri = lax.broadcasted_iota(jnp.int32, (2 * NB, 2 * NB), 0)
+        ci = lax.broadcasted_iota(jnp.int32, (2 * NB, 2 * NB), 1)
+        identity = jnp.where(ri == ci, 1.0, 0.0).astype(jnp.float32)
+        energy = jnp.sum(jnp.where((ri == ci) & (ri < NB), hermit, 0.0), axis=(0, 1), keepdims=True) / (3.0 * NB * points)
+
+        def mul(a, b):
+            return jnp.dot(a, b, precision=lax.Precision.HIGHEST, preferred_element_type=jnp.float32)
+
+        iterate = hermit / frob
+        inverse = identity
+        for step in range(NSIT):
+            factor = 1.5 * identity - 0.5 * (iterate if step == 0 else mul(inverse, iterate))
+            if step < NSIT - 1:
+                iterate = mul(iterate, factor)
+                inverse = factor if step == 0 else mul(factor, inverse)
+            else:
+                inverse = mul(factor[:NB], inverse)
+        scaled = inverse[:NB] * jnp.sqrt(6.0 * points / frob)
+        upper = scaled[:, :NB]
+        lower = scaled[:, NB:]
+        msg[:NB, :] = jnp.concatenate([upper, -lower, lower, upper], axis=1).astype(jnp.bfloat16)
+        high = energy.astype(jnp.bfloat16).astype(jnp.float32)
+        lane = lax.broadcasted_iota(jnp.int32, (16, 128), 1)
+        tail = jnp.where(lane == 0, high, jnp.where(lane == 1, energy - high, 0.0))
+        msg[NB:, :] = tail.astype(jnp.bfloat16)
+        crecv[f_mine] = msg[...]
+
+        @pl.loop(1, total)
+        def _(k):
+            coef_to((lin + k) % total).start()
+
+    for f in range(NF):
+        @pl.when(lin != f * stride)
+        def _(f=f):
+            pltpu.make_async_remote_copy(
+                src_ref=msg, dst_ref=crecv.at[f], send_sem=csend.at[f], recv_sem=crcv.at[f],
+                device_id=where_is(f * stride), device_id_type=MESH).wait_recv()
+
+        pairs = crecv[f, :NB, :]
+        stacked = jnp.concatenate([pairs[:, : 2 * NB], pairs[:, 2 * NB :]], axis=0)
+        tiled = jnp.concatenate([stacked] * 3, axis=1)
+        full = jnp.dot(spread_ref[...], tiled, preferred_element_type=jnp.float32)
+        full = (full * mask_ref[...]).astype(jnp.bfloat16)
+        modes_ref[f * 6 * NB : (f + 1) * 6 * NB, :] = jnp.dot(
+            full, spec[f], preferred_element_type=jnp.float32).astype(jnp.bfloat16)
+        tail = crecv[f, NB:, :].astype(jnp.float32)
+        energy_ref[f : f + 1, :] = jnp.broadcast_to(jnp.sum(tail[:1, :], axis=1, keepdims=True), (1, 128))
+
+    for slot in range(2):
+        for devs, make in ((left[slot], to_left), (right[slot], to_right)):
+            if devs:
+                @pl.when(within(tm, devs))
+                def _(make=make, slot=slot):
+                    make(slot).wait_send()
+
+    @pl.loop(1, n)
+    def _(k):
+        for block in range(per):
+            scatter(block, k).wait_send()
+
+    for f in range(NF):
+        @pl.when(lin != f * stride)
+        def _(f=f):
+            to_owner(f).wait_send()
+
+    @pl.when(lin % stride == 0)
+    def _():
+        @pl.loop(1, total)
+        def _(k):
+            coef_to((lin + k) % total).wait_send()
+
+
+def fused(n, nf_dev, chosen, snapshots, block_starts, freq_index):
+    per, left, right = chosen
+    rows, count, wide = snapshots.shape
+    total = n * nf_dev
+    tables = shifted_tables(block_starts, freq_index, n, per, rows)
+    spread, mask = expanders()
+    pw = wide // n
+    f32, bf16 = jnp.float32, jnp.bfloat16
+    dma = pltpu.SemaphoreType.DMA
+    vmem = pl.BlockSpec(memory_space=pltpu.VMEM)
+    modes, energy = pl.pallas_call(
+        functools.partial(kernel, n, nf_dev, per, left, right, float(wide * nf_dev)),
+        out_shape=(jax.ShapeDtypeStruct((NF * NB * 6, pw), bf16), jax.ShapeDtypeStruct((NF, 128), f32)),
+        in_specs=[pl.BlockSpec(memory_space=pl.ANY), vmem, vmem, vmem],
+        out_specs=(vmem, vmem),
+        scratch_shapes=[
+            pltpu.VMEM((3, rows, wide), bf16),
+            pltpu.VMEM((2, ROWS, 3 * wide), f32),
+            pltpu.VMEM((2, ROWS, 3 * wide), f32),
+            pltpu.VMEM((2, ROWS, 3 * wide), f32),
+            pltpu.VMEM((2, ROWS, 3 * wide), f32),
+            pltpu.VMEM((per * ROWS, 3 * wide), f32),
+            pltpu.VMEM((n, per, ROWS, 3 * pw), bf16),
+            pltpu.VMEM((n, per, ROWS, 3 * pw), bf16),
+            pltpu.VMEM((3, NB * ROWS, pw), f32),
+            pltpu.VMEM((NF, 6 * NB, pw), bf16),
+            pltpu.VMEM((NF, NB // 2, 4 * NB), f32),
+            pltpu.VMEM((total, NB // 2, 4 * NB), f32),
+            pltpu.VMEM((NB + 16, 4 * NB), bf16),
+            pltpu.VMEM((NF, NB + 16, 4 * NB), bf16),
+            dma((3,)), dma((2,)), dma((2,)), dma((2,)), dma((2,)),
+            dma((per, n)), dma((per, n)), dma((NF,)), dma((total,)), dma((total,)), dma((NF,)),
+        ],
+        compiler_params=pltpu.CompilerParams(
+            collective_id=0, has_side_effects=True, vmem_limit_bytes=48 * 1024 * 1024),
+    )(jnp.transpose(snapshots, (1, 0, 2)), tables, spread, mask)
+    modes = modes.reshape(NF, NB, 3, 2, pw).transpose(0, 1, 3, 2, 4)
+    return modes, energy[:, 0]
+
+
 def solution(mesh):
+    n, nf_dev = mesh.shape["tm"], mesh.shape["freq"]
+
+    def body(snapshots, block_starts, freq_index):
+        rows, _, wide = snapshots.shape
+        chosen = plan(n, rows, n * nf_dev, wide // n)
+        if chosen is None:
+            return local(snapshots, block_starts, freq_index)
+        return fused(n, nf_dev, chosen, snapshots, block_starts, freq_index)
+
     return jax.shard_map(
-        local,
+        body,
         mesh=mesh,
         in_specs=(P("tm", None, "freq"), P(), P()),
         out_specs=(P(None, None, None, None, ("freq", "tm")), P()),

time: 303 us -> 80 us (0.26)
  waiting for transfers between devices: 145 us -> 0 us
  Pallas kernels: 0 us -> 66.5 us
  local copies, waits for them, and re-layouts: 67.9 us -> 5.08 us
  blocking collectives: 51.9 us -> 0 us
  between operations: 16.4 us -> 1.43 us
  matrix products: 10.8 us -> 0 us
  starting transfers between devices: 7.49 us -> 0 us
  other arithmetic: 2.93 us -> 6.22 us
    all_to_all x1 -> x0, waiting for transfers between devices: 112 us -> none  [local(): lax.all_to_all(snapshots, 'tm', split_axis=2, concat_axis=0, tiled=True)]
    pallas_call x0 -> x1, Pallas kernels: none -> 66.5 us  [fused(): pl.pallas_call(functools.partial(kernel, n, nf_dev, per, left, right, flo...]
    psum x1 -> x0, blocking collectives: 38.6 us -> none  [local(): shared = lax.psum(shared, 'tm')]
    unnamed x2 -> x0, waiting for transfers between devices: 32.6 us -> none
    gather x1, local copies, waits for them, and re-layouts: 33.1 us -> 0.64 us  [shifted_tables(): starts = jnp.take(block_starts, jnp.clip(ids, 0, NB - 1))]
    reshape x3 -> x0, local copies, waits for them, and re-layouts: 13.3 us -> none  [the longest x2 13 us: local(): columns_all = series.reshape(series.shape[0], count * width)]
    dot_general x22 -> x0, matrix products: 10.8 us -> none  [the longest x17 4.63 us: matmul_batch(): jnp.einsum('fij,fjk->fik', left, right, precision=lax.Precision.HIGHEST)]
    unnamed x13 -> x5, local copies, waits for them, and re-layouts: 12.5 us -> 2.83 us
  transfers between devices with their start and end apart: 2 -> 0, of which waited for: 2 -> 0; matrix products, arithmetic and copies ran while one was open for 1% -> 0% of each run, Pallas kernels for 0% -> 0%
where the time goes in v1:
time: 80 us; the launch traced here: 79.3 us
  Pallas kernels  66.5 us (83%)
  other arithmetic  6.22 us (8%)
  local copies, waits for them, and re-layouts  5.08 us (6%)
  between operations  1.43 us (2%)
    pallas_call x1, Pallas kernels, fused(): pl.pallas_call(functools.partial(kernel, n, nf_dev, per, left, right, flo...  66.5 us
    convert_element_type x1, other arithmetic, shifted_tables(): return table.reshape((per + 4) * ROWS, rows).astype(jnp.bfloat16)  3.09 us
    unnamed x5, local copies, waits for them, and re-layouts  2.83 us

profile of v1, /device:TPU:0, one launch (start us, length us, event | category | flops | bytes accessed | tf_op | source)
XLA Modules:
  0.0 79.3 jit_solution(12649250851914775594)
XLA Ops:
  0.6 0.0 copy-start
  0.6 0.6 multiply_reduce_fusion
  2.0 0.7 compare_and_fusion
  2.7 0.7 compare_select_fusion
  3.3 0.1 broadcast_in_dim.40
  3.5 0.0 copy-done
  3.5 0.6 gather_fusion
  4.1 0.7 and_select_fusion.8
  4.8 0.7 broadcast_in_dim.42
  5.5 0.1 mul.81
  5.6 0.1 mul.83
  5.7 0.1 subtract_select_fusion
  5.8 0.2 subtract_select_fusion.1
  6.0 0.1 and_convert_fusion.spread_ref
  6.1 0.1 compare_convert_fusion.mask_ref
  6.2 3.1 %fusion.6.t_ref = bf16[256,544]{1,0:T(8,128)(2,1)S(1)} fusion(f32[]{:T(128)S(6)} %sqrt.3, s32[8,544]{1,0:T(8,128)S(1)} %subtract_select_fusion, s32[256]{0:T(256)S(1)} %mul.83, f32[8,544]{1,0:T(8,128)S(1)} %subtract_select_fusion.1, pred[256]{0:T(512)(128)(4,1)S(1)} %broadcast_in_dim.40), kind=kLoop, calls=%fused_computation.12 | loop fusion | flops 2646016 | bytes 314628 | tf_op jit(solution)/shard_map/convert_element_type | solution.py:155
  9.3 0.0 copy-start.1
  9.3 1.9 %copy-done.1 = bf16[544,3,1024]{2,0,1:T(8,128)(2,1)S(1)} copy-done((bf16[544,3,1024]{2,0,1:T(8,128)(2,1)S(1)}, bf16[544,3,1024]{2,0,1:T(8,128)(2,1)}, u32[]{:S(2)}) %copy-start.1) | copy-done | bytes 3342360
  11.2 66.5 %shard_map.59 = (bf16[3072,128]{1,0:T(8,128)(2,1)S(1)}, f32[16,128]{1,0:T(8,128)S(1)}) custom-call(bf16[3,544,1024]{2,1,0:T(8,128)(2,1)S(1)} %bitcast.28, bf16[256,544]{1,0:T(8,128)(2,1)S(1)} %fusion.6.t_ref, bf16[192,64]{1,0:T(8,128)(2,1)S(1)} %and_convert_fusion.spread_ref, f32[192,192]{1,0:T(8,128)S(1)} %compare_convert_fusion.mask_ref), custom_call_target="tpu_custom_call" | custom-call | tf_op jit(solution)/shard_map/pallas_call | solution.py:401
  77.8 0.6 slice_reduce_fusion
  78.4 0.9 %copy.7 = bf16[16,32,2,3,128]{4,2,3,1,0:T(2,128)(2,1)} copy(bf16[16,32,2,3,128]{4,2,3,1,0:T(2,128)(2,1)S(1)} %bitcast.29) | data formatting | bytes 1572864
  (8 shorter events, 0.0 us)
Async XLA Ops:
  0.6 2.9 %copy-start = (s32[32]{0:T(128)S(1)}, s32[32]{0:T(128)}, u32[]{:S(2)}) copy-start(s32[32]{0:T(128)} %param.5) | copy-start | bytes 388
  9.3 1.9 %copy-start.1 = (bf16[544,3,1024]{2,0,1:T(8,128)(2,1)S(1)}, bf16[544,3,1024]{2,0,1:T(8,128)(2,1)}, u32[]{:S(2)}) copy-start(bf16[544,3,1024]{2,0,1:T(8,128)(2,1)} %param.4) | copy-start | bytes 10027012

commit v2 on v1

--- a/solution.py
+++ b/solution.py
@@ -3,6 +3,7 @@
 
 import jax
 import jax.numpy as jnp
+import numpy as np
 from jax import lax
 from jax.experimental import pallas as pl
 from jax.experimental.pallas import tpu as pltpu
@@ -133,43 +134,49 @@
     return per, left, right
 
 
-def shifted_tables(block_starts, freq_index, n, per, rows):
-    me = lax.axis_index("tm")
-    offsets = jnp.array([-1, -2, per, per + 1] + list(range(per)), dtype=jnp.int32)
-    ids = per * me + offsets
-    starts = jnp.take(block_starts, jnp.clip(ids, 0, NB - 1))
-    local_t = rows * me + jnp.arange(rows, dtype=jnp.int32)[None, :] - starts[:, None]
-    inside = (local_t >= 0) & (local_t < NFFT) & ((ids >= 0) & (ids < NB))[:, None]
-    local_t = jnp.where(inside, local_t, 0)
-    times_idx = jnp.arange(NFFT, dtype=jnp.int32)
-    full_window = 0.5 - 0.5 * jnp.cos(2.0 * math.pi / NFFT * times_idx.astype(jnp.float32))
-    scaling = 1.0 / jnp.sqrt(jnp.sum(full_window * full_window))
-    window = 0.5 - 0.5 * jnp.cos(2.0 * math.pi / NFFT * local_t.astype(jnp.float32))
-    window = jnp.where(inside, window, 0.0)
-    freqs = jnp.repeat(freq_index, 2)
-    phase = freqs[None, :, None] * local_t[:, None, :] % NFFT
+def base_table(freq_ref):
+    row = lax.broadcasted_iota(jnp.int32, (ROWS, NFFT), 0)
+    times_idx = lax.broadcasted_iota(jnp.int32, (ROWS, NFFT), 1)
+    freqs = jnp.zeros((ROWS, NFFT), jnp.int32)
+    for f in range(NF):
+        freqs = jnp.where((row >> 1) == f, freq_ref[f], freqs)
+    phase = (freqs * times_idx) & (NFFT - 1)
     angles = 2.0 * math.pi / NFFT * phase.astype(jnp.float32)
-    is_sine = (jnp.arange(ROWS) % 2 == 1)[None, :, None]
-    wave = jnp.where(is_sine, -jnp.sin(angles), jnp.cos(angles))
-    table = window[:, None, :] * wave * scaling
-    return table.reshape((per + 4) * ROWS, rows).astype(jnp.bfloat16)
-
-
-def expanders():
-    row = jnp.arange(NB * 6)
-    col = jnp.arange(2 * NB)
-    spread = (row[:, None] // 6 == col[None, :] % NB) & (row[:, None] % 2 == col[None, :] // NB)
-    wide = jnp.arange(3 * 2 * NB)
-    mask = row[:, None] // 2 % 3 == wide[None, :] // (2 * NB)
-    return spread.astype(jnp.bfloat16), mask.astype(jnp.float32)
+    window = 0.5 - 0.5 * jnp.cos(2.0 * math.pi / NFFT * times_idx.astype(jnp.float32))
+    hann = 0.5 - 0.5 * np.cos(2.0 * math.pi / NFFT * np.arange(NFFT))
+    scaling = np.float32(1.0 / np.sqrt(np.sum(hann * hann)))
+    cosine = window * jnp.cos(angles) * scaling
+    sine = -window * jnp.sin(angles) * scaling
+    return jnp.where((row & 1) == 1, sine, cosine).astype(jnp.bfloat16)
+
+
+def shifted(base, shift, rows):
+    source = lax.broadcasted_iota(jnp.int32, (NFFT, rows), 0)
+    target = lax.broadcasted_iota(jnp.int32, (NFFT, rows), 1)
+    pick = jnp.where(source - target == shift, 1.0, 0.0).astype(jnp.bfloat16)
+    return jnp.dot(base, pick, preferred_element_type=jnp.float32).astype(jnp.bfloat16)
+
+
+def expanders(spread_ref, mask_ref):
+    row = lax.broadcasted_iota(jnp.int32, (NB * 6, 2 * NB), 0)
+    col = lax.broadcasted_iota(jnp.int32, (NB * 6, 2 * NB), 1)
+    first = 6 * (col & (NB - 1))
+    hit = (row >= first) & (row < first + 6) & ((row & 1) == jnp.where(col >= NB, 1, 0))
+    spread_ref[...] = jnp.where(hit, 1.0, 0.0).astype(jnp.bfloat16)
+    row = lax.broadcasted_iota(jnp.int32, (NB * 6, 6 * NB), 0)
+    col = lax.broadcasted_iota(jnp.int32, (NB * 6, 6 * NB), 1)
+    pair = row >> 1
+    comp = pair - 3 * ((pair * 43691) >> 17)
+    part = jnp.where(col >= 4 * NB, 2, jnp.where(col >= 2 * NB, 1, 0))
+    mask_ref[...] = jnp.where(comp == part, 1.0, 0.0)
 
 
 def within(me, devs):
     return (me >= devs[0]) & (me <= devs[-1])
 
 
-def kernel(n, nf_dev, per, left, right, points, x_hbm, t_ref, spread_ref, mask_ref,
-           modes_ref, energy_ref, xv, out_l, out_r, in_l, in_r, own, sendb, recvb, spec32, spec,
+def kernel(n, nf_dev, per, left, right, points, x_hbm, starts_ref, freq_ref,
+           modes_ref, energy_ref, t_ref, spread_ref, mask_ref, xv, out_l, out_r, in_l, in_r, own, sendb, recvb, spec32, spec,
            gpart, gath, msg, crecv, load_sem, lsend, lrecv, rsend, rrecv, asend, arecv,
            gsend, grecv, csend, crcv):
     tm = lax.axis_index("tm")
@@ -189,6 +196,15 @@
     def _(k):
         pl.semaphore_signal(barrier, inc=1, device_id=where_is((lin + k) % total), device_id_type=MESH)
 
+    rows = xv.shape[1]
+    base = base_table(freq_ref)
+    for slot, offset in enumerate([-1, -2, per, per + 1] + list(range(per))):
+        block = per * tm + offset
+        start = starts_ref[jnp.clip(block, 0, NB - 1)]
+        inside = (block >= 0) & (block < NB)
+        shift = jnp.where(inside, rows * tm - start, 4 * (rows + NFFT))
+        t_ref[slot * ROWS : (slot + 1) * ROWS, :] = shifted(base, shift, rows)
+    expanders(spread_ref, mask_ref)
     width = xv.shape[2]
     for c in range(3):
         pltpu.make_async_copy(x_hbm.at[c], xv.at[c], load_sem.at[c]).wait()
@@ -286,10 +302,11 @@
         gram = lax.dot_general(lhs, rhs, (((1,), (1,)), ((), ())), preferred_element_type=jnp.float32)
         half = NB // 2
         gpart[f] = jnp.concatenate([gram[:half], gram[half:]], axis=1)
-
-        @pl.when(lin != f * stride)
-        def _(f=f):
-            to_owner(f).start()
+        if f % 4 == 3:
+            for sent in range(f - 3, f + 1):
+                @pl.when(lin != sent * stride)
+                def _(sent=sent):
+                    to_owner(sent).start()
 
     def coef_to(index):
         return pltpu.make_async_remote_copy(
@@ -354,6 +371,7 @@
                 src_ref=msg, dst_ref=crecv.at[f], send_sem=csend.at[f], recv_sem=crcv.at[f],
                 device_id=where_is(f * stride), device_id_type=MESH).wait_recv()
 
+    for f in range(NF):
         pairs = crecv[f, :NB, :]
         stacked = jnp.concatenate([pairs[:, : 2 * NB], pairs[:, 2 * NB :]], axis=0)
         tiled = jnp.concatenate([stacked] * 3, axis=1)
@@ -392,18 +410,20 @@
     per, left, right = chosen
     rows, count, wide = snapshots.shape
     total = n * nf_dev
-    tables = shifted_tables(block_starts, freq_index, n, per, rows)
-    spread, mask = expanders()
     pw = wide // n
     f32, bf16 = jnp.float32, jnp.bfloat16
     dma = pltpu.SemaphoreType.DMA
     vmem = pl.BlockSpec(memory_space=pltpu.VMEM)
+    smem = pl.BlockSpec(memory_space=pltpu.SMEM)
     modes, energy = pl.pallas_call(
         functools.partial(kernel, n, nf_dev, per, left, right, float(wide * nf_dev)),
         out_shape=(jax.ShapeDtypeStruct((NF * NB * 6, pw), bf16), jax.ShapeDtypeStruct((NF, 128), f32)),
-        in_specs=[pl.BlockSpec(memory_space=pl.ANY), vmem, vmem, vmem],
+        in_specs=[pl.BlockSpec(memory_space=pltpu.HBM), smem, smem],
         out_specs=(vmem, vmem),
         scratch_shapes=[
+            pltpu.VMEM(((per + 4) * ROWS, rows), bf16),
+            pltpu.VMEM((NB * 6, 2 * NB), bf16),
+            pltpu.VMEM((NB * 6, 6 * NB), f32),
             pltpu.VMEM((3, rows, wide), bf16),
             pltpu.VMEM((2, ROWS, 3 * wide), f32),
             pltpu.VMEM((2, ROWS, 3 * wide), f32),
@@ -423,7 +443,7 @@
         ],
         compiler_params=pltpu.CompilerParams(
             collective_id=0, has_side_effects=True, vmem_limit_bytes=48 * 1024 * 1024),
-    )(jnp.transpose(snapshots, (1, 0, 2)), tables, spread, mask)
+    )(jnp.transpose(snapshots, (1, 0, 2)), block_starts, freq_index)
     modes = modes.reshape(NF, NB, 3, 2, pw).transpose(0, 1, 3, 2, 4)
     return modes, energy[:, 0]
 

time: 80 us -> 71.1 us (0.89)
  other arithmetic: 6.22 us -> 0 us
  Pallas kernels: 66.5 us -> 65.6 us
    convert_element_type x3 -> x0, other arithmetic: 3.3 us -> none  [the longest x1 3.09 us: shifted_tables(): return table.reshape((per + 4) * ROWS, rows).astype(jnp.bfloat16)]
    select_n x7 -> x0, other arithmetic: 1.59 us -> none  [the longest x2 1.33 us: shifted_tables(): starts = jnp.take(block_starts, jnp.clip(ids, 0, NB - 1))]
    unnamed x5 -> x7, local copies, waits for them, and re-layouts: 2.83 us -> 4.13 us
    pallas_call x1, Pallas kernels: 66.5 us -> 65.6 us  [fused(): pl.pallas_call(functools.partial(kernel, n, nf_dev, per, left, right, flo...]
    broadcast_in_dim x3 -> x0, local copies, waits for them, and re-layouts: 0.82 us -> none  [the longest x1 0.72 us: shifted_tables(): freqs = jnp.repeat(freq_index, 2)]
where the time goes in v2:
time: 71.1 us; the launch traced here: 71 us
  Pallas kernels  65.6 us (92%)
  local copies, waits for them, and re-layouts  4.75 us (7%)
    pallas_call x1, Pallas kernels, fused(): pl.pallas_call(functools.partial(kernel, n, nf_dev, per, left, right, flo...  65.6 us
    unnamed x7, local copies, waits for them, and re-layouts  4.13 us

profile of v2, /device:TPU:0, one launch (start us, length us, event | category | flops | bytes accessed | tf_op | source)
XLA Modules:
  0.0 71.0 jit_solution(2450913389692873698)
XLA Ops:
  0.6 0.0 copy-start
  0.6 1.9 %copy-done = bf16[544,3,1024]{2,0,1:T(8,128)(2,1)S(1)} copy-done((bf16[544,3,1024]{2,0,1:T(8,128)(2,1)S(1)}, bf16[544,3,1024]{2,0,1:T(8,128)(2,1)}, u32[]{:S(2)}) %copy-start) | copy-done | bytes 3342360
  2.6 0.0 copy-start.1
  2.6 0.7 copy-done.1
  3.2 0.0 copy-start.2
  3.2 0.7 copy-done.2
  3.9 65.6 %shard_map.50 = (bf16[3072,128]{1,0:T(8,128)(2,1)S(1)}, f32[16,128]{1,0:T(8,128)S(1)}) custom-call(bf16[3,544,1024]{2,1,0:T(8,128)(2,1)S(1)} %bitcast.4, s32[32]{0:T(128)S(1)} %copy-done.1, s32[16]{0:T(128)S(1)} %copy-done.2), custom_call_target="tpu_custom_call" | custom-call | tf_op jit(solution)/shard_map/pallas_call | solution.py:418
  69.5 0.6 slice_reduce_fusion
  70.1 0.9 %copy.6 = bf16[16,32,2,3,128]{4,2,3,1,0:T(2,128)(2,1)} copy(bf16[16,32,2,3,128]{4,2,3,1,0:T(2,128)(2,1)S(1)} %bitcast.5) | data formatting | bytes 1572864
Async XLA Ops:
  0.6 1.9 %copy-start = (bf16[544,3,1024]{2,0,1:T(8,128)(2,1)S(1)}, bf16[544,3,1024]{2,0,1:T(8,128)(2,1)}, u32[]{:S(2)}) copy-start(bf16[544,3,1024]{2,0,1:T(8,128)(2,1)} %param.3) | copy-start | bytes 10027012
  2.6 0.7 copy-start.1
  3.2 0.7 copy-start.2

commit v3 on v2

--- a/solution.py
+++ b/solution.py
@@ -108,30 +108,34 @@
 
 
 def plan(n, rows, total, width):
-    if n < 2 or NB % n or total % NF or total // NF < 1 or width != 128 or rows % 16:
+    if n < 2 or n % 2 or NB % n or total % NF or width != 128 or rows % 16:
         return None
     per = NB // n
-    if per < 4:
+    if per < 4 or per % 2:
         return None
-    left, right = [[], []], [[], []]
-    for dev in range(n):
-        first, end = rows * dev, rows * (dev + 1)
-        for block in range(NB):
-            if HOP * block >= end or HOP * block + JIT + NFFT <= first:
-                continue
-            owner = block // per
-            if owner == dev:
-                continue
-            if owner == dev - 1 and per * dev - block <= 2:
-                left[per * dev - block - 1].append(dev)
-            elif owner == dev + 1 and block - per * (dev + 1) < 2:
-                right[block - per * (dev + 1)].append(dev)
+    slots = per + 4
+    whole = [[] for _ in range(slots)]
+    shared = [[] for _ in range(slots)]
+    holders = []
+    for block in range(NB):
+        touched = [
+            dev for dev in range(n)
+            if HOP * block < rows * (dev + 1) and HOP * block + JIT + NFFT > rows * dev
+        ]
+        holders.append(touched)
+        if len(touched) > 2:
+            return None
+        for dev in touched:
+            slot = block - per * dev + 2
+            if not 0 <= slot < slots:
+                return None
+            if len(touched) == 2:
+                if (slot < slots // 2) != (dev == touched[1]):
+                    return None
+                shared[slot].append(dev)
             else:
-                return None
-    for devs in left + right:
-        if devs and devs != list(range(devs[0], devs[-1] + 1)):
-            return None
-    return per, left, right
+                whole[slot].append(dev)
+    return per, whole, shared, holders
 
 
 def base_table(freq_ref):
@@ -171,23 +175,39 @@
     mask_ref[...] = jnp.where(comp == part, 1.0, 0.0)
 
 
-def within(me, devs):
-    return (me >= devs[0]) & (me <= devs[-1])
-
-
-def kernel(n, nf_dev, per, left, right, points, x_hbm, starts_ref, freq_ref,
-           modes_ref, energy_ref, t_ref, spread_ref, mask_ref, xv, out_l, out_r, in_l, in_r, own, sendb, recvb, spec32, spec,
-           gpart, gath, msg, crecv, load_sem, lsend, lrecv, rsend, rrecv, asend, arecv,
-           gsend, grecv, csend, crcv):
+def member(index, devs):
+    if not devs:
+        return None
+    if devs == list(range(devs[0], devs[-1] + 1)):
+        return (index >= devs[0]) & (index <= devs[-1])
+    hit = index == devs[0]
+    for dev in devs[1:]:
+        hit = hit | (index == dev)
+    return hit
+
+
+def kernel(n, nf_dev, per, whole, shared, holders, points, x_hbm, starts_hbm, freq_hbm,
+           modes_ref, energy_ref, starts_ref, freq_ref, t_ref, spread_ref, mask_ref, xv, parts,
+           others, sendb, recvb, spec32, spec, gpart, gath, msg, crecv, load_sem, psend, precv,
+           asend, arecv, gsend, grecv, csend, crcv):
     tm = lax.axis_index("tm")
     fr = lax.axis_index("freq")
     total = n * nf_dev
     lin = tm * nf_dev + fr
     stride = total // NF
+    slots = per + 4
+    half_n = n // 2
+    parity = tm % 2
 
     def where_is(index):
         return {"tm": index // nf_dev, "freq": index % nf_dev}
 
+    small = [
+        pltpu.make_async_copy(starts_hbm, starts_ref, load_sem.at[3]),
+        pltpu.make_async_copy(freq_hbm, freq_ref, load_sem.at[4]),
+    ]
+    for copy in small:
+        copy.start()
     for c in range(3):
         pltpu.make_async_copy(x_hbm.at[c], xv.at[c], load_sem.at[c]).start()
     barrier = pltpu.get_barrier_semaphore()
@@ -196,95 +216,121 @@
     def _(k):
         pl.semaphore_signal(barrier, inc=1, device_id=where_is((lin + k) % total), device_id_type=MESH)
 
+    for copy in small:
+        copy.wait()
     rows = xv.shape[1]
     base = base_table(freq_ref)
-    for slot, offset in enumerate([-1, -2, per, per + 1] + list(range(per))):
-        block = per * tm + offset
+    for slot in range(slots):
+        block = per * tm + slot - 2
         start = starts_ref[jnp.clip(block, 0, NB - 1)]
         inside = (block >= 0) & (block < NB)
         shift = jnp.where(inside, rows * tm - start, 4 * (rows + NFFT))
         t_ref[slot * ROWS : (slot + 1) * ROWS, :] = shifted(base, shift, rows)
     expanders(spread_ref, mask_ref)
     width = xv.shape[2]
+    pw = width // n
     for c in range(3):
         pltpu.make_async_copy(x_hbm.at[c], xv.at[c], load_sem.at[c]).wait()
-        part = jnp.dot(t_ref[: 4 * ROWS, :], xv[c], preferred_element_type=jnp.float32)
-        for slot in range(2):
-            out_l[slot, :, c * width : (c + 1) * width] = part[slot * ROWS : (slot + 1) * ROWS]
-            out_r[slot, :, c * width : (c + 1) * width] = part[(slot + 2) * ROWS : (slot + 3) * ROWS]
+        part = jnp.dot(t_ref[...], xv[c], preferred_element_type=jnp.float32)
+        for slot in range(slots):
+            for dest in range(n):
+                at = (c * half_n + dest // 2) * pw
+                parts[slot, dest % 2, :, at : at + pw] = part[
+                    slot * ROWS : (slot + 1) * ROWS, dest * pw : (dest + 1) * pw]
     pl.semaphore_wait(barrier, total - 1)
 
-    def to_left(slot):
+    def exchange(slot):
+        low = slot < slots // 2
         return pltpu.make_async_remote_copy(
-            src_ref=out_l.at[slot], dst_ref=in_r.at[slot], send_sem=lsend.at[slot],
-            recv_sem=lrecv.at[slot], device_id={"tm": (tm + n - 1) % n, "freq": fr},
+            src_ref=parts.at[slot, 1 - parity], dst_ref=others.at[slot + per if low else slot - per],
+            send_sem=psend.at[slot], recv_sem=precv.at[slot + per if low else slot - per],
+            device_id={"tm": (tm + n - 1) % n if low else (tm + 1) % n, "freq": fr},
             device_id_type=MESH)
 
-    def to_right(slot):
+    def arrival(slot):
         return pltpu.make_async_remote_copy(
-            src_ref=out_r.at[slot], dst_ref=in_l.at[slot], send_sem=rsend.at[slot],
-            recv_sem=rrecv.at[slot], device_id={"tm": (tm + 1) % n, "freq": fr},
-            device_id_type=MESH)
-
-    for slot in range(2):
-        for devs, make in ((left[slot], to_left), (right[slot], to_right)):
-            if devs:
-                @pl.when(within(tm, devs))
-                def _(make=make, slot=slot):
-                    make(slot).start()
-
-    for c in range(3):
-        own[:, c * width : (c + 1) * width] = jnp.dot(
-            t_ref[4 * ROWS :, :], xv[c], preferred_element_type=jnp.float32)
-
-    def scatter(block, k):
-        dest = (tm + k) % n
+            src_ref=parts.at[slot, 1 - parity], dst_ref=others.at[slot],
+            send_sem=psend.at[slot], recv_sem=precv.at[slot],
+            device_id={"tm": tm, "freq": fr}, device_id_type=MESH)
+
+    outward = []
+    for step in range(slots // 2):
+        outward += [(slots // 2 + step) % slots, slots // 2 - 1 - step]
+    inward = [slot + per if slot < slots // 2 else slot - per for slot in outward]
+
+    for slot in outward:
+        if shared[slot]:
+            @pl.when(member(tm, shared[slot]))
+            def _(slot=slot):
+                exchange(slot).start()
+
+    def scatter(slot, dest):
         return pltpu.make_async_remote_copy(
-            src_ref=sendb.at[dest, block], dst_ref=recvb.at[tm, block],
-            send_sem=asend.at[block, dest], recv_sem=arecv.at[block, tm],
+            src_ref=sendb.at[slot, dest], dst_ref=recvb.at[per * tm + slot - 2],
+            send_sem=asend.at[slot, dest], recv_sem=arecv.at[per * tm + slot - 2],
             device_id={"tm": dest, "freq": fr}, device_id_type=MESH)
 
-    order = list(range(2, per - 2)) + [1, per - 2, per - 1, 0]
-    for block in order:
-        span = slice(block * ROWS, (block + 1) * ROWS)
-        if block < 2 and right[block]:
-            @pl.when(within(tm - 1, right[block]))
-            def _(block=block, span=span):
-                to_right(block).wait_recv()
-                own[span, :] += in_l[block]
-        back = per - 1 - block
-        if back < 2 and left[back]:
-            @pl.when(within(tm + 1, left[back]))
-            def _(back=back, span=span):
-                to_left(back).wait_recv()
-                own[span, :] += in_r[back]
-        pw = width // n
-        for dest in range(n):
+    def same_side(k):
+        return 2 * ((tm // 2 + k) % half_n) + parity
+
+    def other_side(k):
+        return 2 * ((tm // 2 + k) % half_n) + 1 - parity
+
+    def finish(slot, side, add):
+        for q in range(half_n):
             for c in range(3):
-                sendb[dest, block, :, c * pw : (c + 1) * pw] = own[
-                    span, c * width + dest * pw : c * width + (dest + 1) * pw].astype(jnp.bfloat16)
-
-        @pl.loop(1, n)
-        def _(k, block=block):
-            scatter(block, k).start()
-
-    def widen(src, block, values):
-        base = (src * per + block) * ROWS
+                at = (c * half_n + q) * pw
+                value = parts[slot, side, :, at : at + pw]
+                if add:
+                    value = value + others[slot, :, at : at + pw]
+                sendb[slot, 2 * q + side, :, c * pw : (c + 1) * pw] = value.astype(jnp.bfloat16)
+
+    def keep(slot):
+        recvb[per * tm + slot - 2] = sendb[slot, tm]
+
+    for slot in range(slots):
+        if whole[slot]:
+            @pl.when(member(tm, whole[slot]))
+            def _(slot=slot):
+                finish(slot, parity, False)
+                finish(slot, 1 - parity, False)
+
+                @pl.loop(1, half_n)
+                def _(k):
+                    scatter(slot, same_side(k)).start()
+
+                @pl.loop(0, half_n)
+                def _(k):
+                    scatter(slot, other_side(k)).start()
+
+                keep(slot)
+
+    for slot in inward:
+        if shared[slot]:
+            @pl.when(member(tm, shared[slot]))
+            def _(slot=slot):
+                arrival(slot).wait_recv()
+                finish(slot, parity, True)
+
+                @pl.loop(1, half_n)
+                def _(k):
+                    scatter(slot, same_side(k)).start()
+
+                keep(slot)
+
+    ordered = [b for b in range(NB) if len(holders[b]) == 1] + [b for b in range(NB) if len(holders[b]) == 2]
+    for block in ordered:
+        @pl.when(jnp.logical_not(member(tm, holders[block])))
+        def _(block=block):
+            pltpu.make_async_remote_copy(
+                src_ref=sendb.at[0, 0], dst_ref=recvb.at[block], send_sem=asend.at[0, 0],
+                recv_sem=arecv.at[block], device_id={"tm": tm, "freq": fr},
+                device_id_type=MESH).wait_recv()
+
+    for block in range(NB):
+        values = recvb[block]
         for c in range(3):
-            spec32[c, pl.ds(pl.multiple_of(base, ROWS), ROWS), :] = values[:, c * 128 : (c + 1) * 128].astype(jnp.float32)
-
-    for block in range(per):
-        widen(tm, block, sendb[tm, block])
-
-    @pl.loop(1, n)
-    def _(k):
-        src = (tm + n - k) % n
-        for block in range(per):
-            pltpu.make_async_remote_copy(
-                src_ref=sendb.at[src, block], dst_ref=recvb.at[src, block],
-                send_sem=asend.at[block, src], recv_sem=arecv.at[block, src],
-                device_id={"tm": src, "freq": fr}, device_id_type=MESH).wait_recv()
-            widen(src, block, recvb[src, block])
+            spec32[c, block * ROWS : (block + 1) * ROWS, :] = values[:, c * 128 : (c + 1) * 128].astype(jnp.float32)
 
     def to_owner(f):
         return pltpu.make_async_remote_copy(
@@ -382,17 +428,26 @@
         tail = crecv[f, NB:, :].astype(jnp.float32)
         energy_ref[f : f + 1, :] = jnp.broadcast_to(jnp.sum(tail[:1, :], axis=1, keepdims=True), (1, 128))
 
-    for slot in range(2):
-        for devs, make in ((left[slot], to_left), (right[slot], to_right)):
-            if devs:
-                @pl.when(within(tm, devs))
-                def _(make=make, slot=slot):
-                    make(slot).wait_send()
-
-    @pl.loop(1, n)
-    def _(k):
-        for block in range(per):
-            scatter(block, k).wait_send()
+    for slot in range(slots):
+        if shared[slot]:
+            @pl.when(member(tm, shared[slot]))
+            def _(slot=slot):
+                exchange(slot).wait_send()
+
+                @pl.loop(1, half_n)
+                def _(k):
+                    scatter(slot, same_side(k)).wait_send()
+
+        if whole[slot]:
+            @pl.when(member(tm, whole[slot]))
+            def _(slot=slot):
+                @pl.loop(1, half_n)
+                def _(k):
+                    scatter(slot, same_side(k)).wait_send()
+
+                @pl.loop(0, half_n)
+                def _(k):
+                    scatter(slot, other_side(k)).wait_send()
 
     for f in range(NF):
         @pl.when(lin != f * stride)
@@ -407,42 +462,41 @@
 
 
 def fused(n, nf_dev, chosen, snapshots, block_starts, freq_index):
-    per, left, right = chosen
+    per, whole, shared, holders = chosen
     rows, count, wide = snapshots.shape
     total = n * nf_dev
     pw = wide // n
+    slots = per + 4
     f32, bf16 = jnp.float32, jnp.bfloat16
     dma = pltpu.SemaphoreType.DMA
     vmem = pl.BlockSpec(memory_space=pltpu.VMEM)
-    smem = pl.BlockSpec(memory_space=pltpu.SMEM)
     modes, energy = pl.pallas_call(
-        functools.partial(kernel, n, nf_dev, per, left, right, float(wide * nf_dev)),
+        functools.partial(kernel, n, nf_dev, per, whole, shared, holders, float(wide * nf_dev)),
         out_shape=(jax.ShapeDtypeStruct((NF * NB * 6, pw), bf16), jax.ShapeDtypeStruct((NF, 128), f32)),
-        in_specs=[pl.BlockSpec(memory_space=pltpu.HBM), smem, smem],
+        in_specs=[pl.BlockSpec(memory_space=pltpu.HBM)] * 3,
         out_specs=(vmem, vmem),
         scratch_shapes=[
-            pltpu.VMEM(((per + 4) * ROWS, rows), bf16),
+            pltpu.SMEM((NB,), jnp.int32),
+            pltpu.SMEM((NF,), jnp.int32),
+            pltpu.VMEM((slots * ROWS, rows), bf16),
             pltpu.VMEM((NB * 6, 2 * NB), bf16),
             pltpu.VMEM((NB * 6, 6 * NB), f32),
             pltpu.VMEM((3, rows, wide), bf16),
-            pltpu.VMEM((2, ROWS, 3 * wide), f32),
-            pltpu.VMEM((2, ROWS, 3 * wide), f32),
-            pltpu.VMEM((2, ROWS, 3 * wide), f32),
-            pltpu.VMEM((2, ROWS, 3 * wide), f32),
-            pltpu.VMEM((per * ROWS, 3 * wide), f32),
-            pltpu.VMEM((n, per, ROWS, 3 * pw), bf16),
-            pltpu.VMEM((n, per, ROWS, 3 * pw), bf16),
+            pltpu.VMEM((slots, 2, ROWS, 3 * wide // 2), f32),
+            pltpu.VMEM((slots, ROWS, 3 * wide // 2), f32),
+            pltpu.VMEM((slots, n, ROWS, 3 * pw), bf16),
+            pltpu.VMEM((NB, ROWS, 3 * pw), bf16),
             pltpu.VMEM((3, NB * ROWS, pw), f32),
             pltpu.VMEM((NF, 6 * NB, pw), bf16),
             pltpu.VMEM((NF, NB // 2, 4 * NB), f32),
             pltpu.VMEM((total, NB // 2, 4 * NB), f32),
             pltpu.VMEM((NB + 16, 4 * NB), bf16),
             pltpu.VMEM((NF, NB + 16, 4 * NB), bf16),
-            dma((3,)), dma((2,)), dma((2,)), dma((2,)), dma((2,)),
-            dma((per, n)), dma((per, n)), dma((NF,)), dma((total,)), dma((total,)), dma((NF,)),
+            dma((5,)), dma((slots,)), dma((slots,)), dma((slots, n)), dma((NB,)),
+            dma((NF,)), dma((total,)), dma((total,)), dma((NF,)),
         ],
         compiler_params=pltpu.CompilerParams(
-            collective_id=0, has_side_effects=True, vmem_limit_bytes=48 * 1024 * 1024),
+            collective_id=0, has_side_effects=True, vmem_limit_bytes=60 * 1024 * 1024),
     )(jnp.transpose(snapshots, (1, 0, 2)), block_starts, freq_index)
     modes = modes.reshape(NF, NB, 3, 2, pw).transpose(0, 1, 3, 2, 4)
     return modes, energy[:, 0]

time: 71.1 us -> 62.9 us (0.88)
  Pallas kernels: 65.6 us -> 58.1 us
  local copies, waits for them, and re-layouts: 4.75 us -> 3.91 us
    pallas_call x1, Pallas kernels: 65.6 us -> 58.1 us  [fused(): pl.pallas_call(functools.partial(kernel, n, nf_dev, per, whole, shared, h...]
    unnamed x7 -> x1, local copies, waits for them, and re-layouts: 4.13 us -> 2.59 us
where the time goes in v3:
time: 62.9 us; the launch traced here: 62.6 us
  Pallas kernels  58.1 us (92%)
  local copies, waits for them, and re-layouts  3.91 us (6%)
  between operations  0.64 us (1%)
    pallas_call x1, Pallas kernels, fused(): pl.pallas_call(functools.partial(kernel, n, nf_dev, per, whole, shared, h...  58.1 us
    unnamed x1, local copies, waits for them, and re-layouts  2.59 us
    slice x1, local copies, waits for them, and re-layouts, fused(): return (modes, energy[:, 0])  1.32 us

profile of v3, /device:TPU:0, one launch (start us, length us, event | category | flops | bytes accessed | tf_op | source)
XLA Modules:
  0.0 62.6 jit_solution(5897937348331262470)
XLA Ops:
  0.6 58.1 %shard_map.50 = (bf16[3072,128]{1,0:T(8,128)(2,1)}, f32[16,128]{1,0:T(8,128)}) custom-call(bf16[3,544,1024]{2,1,0:T(8,128)(2,1)} %bitcast.4, s32[32]{0:T(128)} %starts_hbm.1, s32[16]{0:T(128)} %freq_hbm.1), custom_call_target="tpu_custom_call" | custom-call | tf_op jit(solution)/shard_map/pallas_call | solution.py:473
  58.7 1.3 %slice_reduce_fusion = f32[16]{0:T(128)} fusion(f32[16,128]{1,0:T(8,128)} %get-tuple-element.5), kind=kLoop, calls=%fused_computation | loop fusion | bytes 128 | tf_op jit(solution)/shard_map/slice | solution.py:502
  60.1 2.6 %copy.6 = bf16[16,32,2,3,128]{4,2,3,1,0:T(2,128)(2,1)} copy(bf16[16,32,2,3,128]{4,2,3,1,0:T(2,128)(2,1)} %bitcast.5) | data formatting | bytes 1572864

commit v4 on v3

--- a/solution.py
+++ b/solution.py
@@ -108,7 +108,7 @@
 
 
 def plan(n, rows, total, width):
-    if n < 2 or n % 2 or NB % n or total % NF or width != 128 or rows % 16:
+    if n < 2 or n % 2 or NB % n or total % (2 * NF) or width != 128 or rows % 16:
         return None
     per = NB // n
     if per < 4 or per % 2:
@@ -194,10 +194,15 @@
     fr = lax.axis_index("freq")
     total = n * nf_dev
     lin = tm * nf_dev + fr
-    stride = total // NF
+    step, lowest = total // (2 * NF), total // 4
     slots = per + 4
+    mine = (lin - lowest) // step
+    owns = (lin >= lowest) & (lin < lowest + NF * step) & ((lin - lowest) % step == 0)
     half_n = n // 2
     parity = tm % 2
+
+    def owner(f):
+        return lowest + f * step
 
     def where_is(index):
         return {"tm": index // nf_dev, "freq": index % nf_dev}
@@ -229,40 +234,41 @@
     expanders(spread_ref, mask_ref)
     width = xv.shape[2]
     pw = width // n
+    def exchange(slot, c):
+        low = slot < slots // 2
+        there = slot + per if low else slot - per
+        return pltpu.make_async_remote_copy(
+            src_ref=parts.at[slot, 1 - parity, c], dst_ref=others.at[there, c],
+            send_sem=psend.at[slot, c], recv_sem=precv.at[there, c],
+            device_id={"tm": (tm + n - 1) % n if low else (tm + 1) % n, "freq": fr},
+            device_id_type=MESH)
+
+    def arrival(slot, c):
+        return pltpu.make_async_remote_copy(
+            src_ref=parts.at[slot, 1 - parity, c], dst_ref=others.at[slot, c],
+            send_sem=psend.at[slot, c], recv_sem=precv.at[slot, c],
+            device_id={"tm": tm, "freq": fr}, device_id_type=MESH)
+
+    outward = []
+    for reach in range(slots // 2):
+        outward += [slots // 2 + reach, slots // 2 - 1 - reach]
+    inward = [slot + per if slot < slots // 2 else slot - per for slot in outward]
+
+    pl.semaphore_wait(barrier, total - 1)
+
     for c in range(3):
         pltpu.make_async_copy(x_hbm.at[c], xv.at[c], load_sem.at[c]).wait()
         part = jnp.dot(t_ref[...], xv[c], preferred_element_type=jnp.float32)
         for slot in range(slots):
             for dest in range(n):
-                at = (c * half_n + dest // 2) * pw
-                parts[slot, dest % 2, :, at : at + pw] = part[
+                at = dest // 2 * pw
+                parts[slot, dest % 2, c, :, at : at + pw] = part[
                     slot * ROWS : (slot + 1) * ROWS, dest * pw : (dest + 1) * pw]
-    pl.semaphore_wait(barrier, total - 1)
-
-    def exchange(slot):
-        low = slot < slots // 2
-        return pltpu.make_async_remote_copy(
-            src_ref=parts.at[slot, 1 - parity], dst_ref=others.at[slot + per if low else slot - per],
-            send_sem=psend.at[slot], recv_sem=precv.at[slot + per if low else slot - per],
-            device_id={"tm": (tm + n - 1) % n if low else (tm + 1) % n, "freq": fr},
-            device_id_type=MESH)
-
-    def arrival(slot):
-        return pltpu.make_async_remote_copy(
-            src_ref=parts.at[slot, 1 - parity], dst_ref=others.at[slot],
-            send_sem=psend.at[slot], recv_sem=precv.at[slot],
-            device_id={"tm": tm, "freq": fr}, device_id_type=MESH)
-
-    outward = []
-    for step in range(slots // 2):
-        outward += [(slots // 2 + step) % slots, slots // 2 - 1 - step]
-    inward = [slot + per if slot < slots // 2 else slot - per for slot in outward]
-
-    for slot in outward:
-        if shared[slot]:
-            @pl.when(member(tm, shared[slot]))
-            def _(slot=slot):
-                exchange(slot).start()
+        for slot in outward:
+            if shared[slot]:
+                @pl.when(member(tm, shared[slot]))
+                def _(slot=slot, c=c):
+                    exchange(slot, c).start()
 
     def scatter(slot, dest):
         return pltpu.make_async_remote_copy(
@@ -279,10 +285,10 @@
     def finish(slot, side, add):
         for q in range(half_n):
             for c in range(3):
-                at = (c * half_n + q) * pw
-                value = parts[slot, side, :, at : at + pw]
+                at = q * pw
+                value = parts[slot, side, c, :, at : at + pw]
                 if add:
-                    value = value + others[slot, :, at : at + pw]
+                    value = value + others[slot, c, :, at : at + pw]
                 sendb[slot, 2 * q + side, :, c * pw : (c + 1) * pw] = value.astype(jnp.bfloat16)
 
     def keep(slot):
@@ -309,7 +315,8 @@
         if shared[slot]:
             @pl.when(member(tm, shared[slot]))
             def _(slot=slot):
-                arrival(slot).wait_recv()
+                for c in range(3):
+                    arrival(slot, c).wait_recv()
                 finish(slot, parity, True)
 
                 @pl.loop(1, half_n)
@@ -335,7 +342,7 @@
     def to_owner(f):
         return pltpu.make_async_remote_copy(
             src_ref=gpart.at[f], dst_ref=gath.at[lin], send_sem=gsend.at[f],
-            recv_sem=grecv.at[lin], device_id=where_is(f * stride), device_id_type=MESH)
+            recv_sem=grecv.at[lin], device_id=where_is(owner(f)), device_id_type=MESH)
 
     for f in range(NF):
         real = [spec32[c, pl.ds(2 * f, NB, stride=ROWS), :].astype(jnp.bfloat16) for c in range(3)]
@@ -350,19 +357,18 @@
         gpart[f] = jnp.concatenate([gram[:half], gram[half:]], axis=1)
         if f % 4 == 3:
             for sent in range(f - 3, f + 1):
-                @pl.when(lin != sent * stride)
+                @pl.when(lin != owner(sent))
                 def _(sent=sent):
                     to_owner(sent).start()
 
     def coef_to(index):
         return pltpu.make_async_remote_copy(
-            src_ref=msg, dst_ref=crecv.at[lin // stride], send_sem=csend.at[index],
-            recv_sem=crcv.at[lin // stride], device_id=where_is(index), device_id_type=MESH)
-
-    @pl.when(lin % stride == 0)
+            src_ref=msg, dst_ref=crecv.at[mine], send_sem=csend.at[index],
+            recv_sem=crcv.at[mine], device_id=where_is(index), device_id_type=MESH)
+
+    @pl.when(owns)
     def _():
-        f_mine = lin // stride
-        gath[lin] = gpart[f_mine]
+        gath[lin] = gpart[mine]
 
         @pl.loop(1, total)
         def _(k):
@@ -397,42 +403,23 @@
             else:
                 inverse = mul(factor[:NB], inverse)
         scaled = inverse[:NB] * jnp.sqrt(6.0 * points / frob)
-        upper = scaled[:, :NB]
-        lower = scaled[:, NB:]
-        msg[:NB, :] = jnp.concatenate([upper, -lower, lower, upper], axis=1).astype(jnp.bfloat16)
+        msg[:16, :] = jnp.concatenate([scaled[:16], scaled[16:]], axis=1).astype(jnp.bfloat16)
         high = energy.astype(jnp.bfloat16).astype(jnp.float32)
         lane = lax.broadcasted_iota(jnp.int32, (16, 128), 1)
         tail = jnp.where(lane == 0, high, jnp.where(lane == 1, energy - high, 0.0))
-        msg[NB:, :] = tail.astype(jnp.bfloat16)
-        crecv[f_mine] = msg[...]
+        msg[16:, :] = tail.astype(jnp.bfloat16)
+        crecv[mine] = msg[...]
 
         @pl.loop(1, total)
         def _(k):
             coef_to((lin + k) % total).start()
-
-    for f in range(NF):
-        @pl.when(lin != f * stride)
-        def _(f=f):
-            pltpu.make_async_remote_copy(
-                src_ref=msg, dst_ref=crecv.at[f], send_sem=csend.at[f], recv_sem=crcv.at[f],
-                device_id=where_is(f * stride), device_id_type=MESH).wait_recv()
-
-    for f in range(NF):
-        pairs = crecv[f, :NB, :]
-        stacked = jnp.concatenate([pairs[:, : 2 * NB], pairs[:, 2 * NB :]], axis=0)
-        tiled = jnp.concatenate([stacked] * 3, axis=1)
-        full = jnp.dot(spread_ref[...], tiled, preferred_element_type=jnp.float32)
-        full = (full * mask_ref[...]).astype(jnp.bfloat16)
-        modes_ref[f * 6 * NB : (f + 1) * 6 * NB, :] = jnp.dot(
-            full, spec[f], preferred_element_type=jnp.float32).astype(jnp.bfloat16)
-        tail = crecv[f, NB:, :].astype(jnp.float32)
-        energy_ref[f : f + 1, :] = jnp.broadcast_to(jnp.sum(tail[:1, :], axis=1, keepdims=True), (1, 128))
 
     for slot in range(slots):
         if shared[slot]:
             @pl.when(member(tm, shared[slot]))
             def _(slot=slot):
-                exchange(slot).wait_send()
+                for c in range(3):
+                    exchange(slot, c).wait_send()
 
                 @pl.loop(1, half_n)
                 def _(k):
@@ -450,11 +437,36 @@
                     scatter(slot, other_side(k)).wait_send()
 
     for f in range(NF):
-        @pl.when(lin != f * stride)
+        @pl.when(lin != owner(f))
         def _(f=f):
             to_owner(f).wait_send()
 
-    @pl.when(lin % stride == 0)
+    for f in range(NF):
+        @pl.when(lin != owner(f))
+        def _(f=f):
+            pltpu.make_async_remote_copy(
+                src_ref=msg, dst_ref=crecv.at[f], send_sem=csend.at[f], recv_sem=crcv.at[f],
+                device_id=where_is(owner(f)), device_id_type=MESH).wait_recv()
+
+    lanes = lax.broadcasted_iota(jnp.int32, (NB, 2 * NB), 1)
+    signs = jnp.where(lanes < NB, 1.0, -1.0).astype(jnp.bfloat16)
+    wide_lane = lax.broadcasted_iota(jnp.int32, (1, NF), 1)
+    energies = jnp.zeros((1, NF), jnp.float32)
+    for f in range(NF):
+        pairs = crecv[f, :16, :]
+        straight = jnp.concatenate([pairs[:, : 2 * NB], pairs[:, 2 * NB :]], axis=0)
+        crossed = jnp.concatenate([straight[:, NB:], straight[:, :NB]], axis=1)
+        stacked = jnp.concatenate([straight * signs, crossed], axis=0)
+        tiled = jnp.concatenate([stacked] * 3, axis=1)
+        full = jnp.dot(spread_ref[...], tiled, preferred_element_type=jnp.float32)
+        full = (full * mask_ref[...]).astype(jnp.bfloat16)
+        modes_ref[f * 6 * NB : (f + 1) * 6 * NB, :] = jnp.dot(
+            full, spec[f], preferred_element_type=jnp.float32).astype(jnp.bfloat16)
+        tail = crecv[f, 16:, :].astype(jnp.float32)
+        energies = jnp.where(wide_lane == f, jnp.sum(tail[:1, :], axis=1, keepdims=True), energies)
+    energy_ref[...] = energies
+
+    @pl.when(owns)
     def _():
         @pl.loop(1, total)
         def _(k):
@@ -472,7 +484,7 @@
     vmem = pl.BlockSpec(memory_space=pltpu.VMEM)
     modes, energy = pl.pallas_call(
         functools.partial(kernel, n, nf_dev, per, whole, shared, holders, float(wide * nf_dev)),
-        out_shape=(jax.ShapeDtypeStruct((NF * NB * 6, pw), bf16), jax.ShapeDtypeStruct((NF, 128), f32)),
+        out_shape=(jax.ShapeDtypeStruct((NF * NB * 6, pw), bf16), jax.ShapeDtypeStruct((1, NF), f32)),
         in_specs=[pl.BlockSpec(memory_space=pltpu.HBM)] * 3,
         out_specs=(vmem, vmem),
         scratch_shapes=[
@@ -482,24 +494,24 @@
             pltpu.VMEM((NB * 6, 2 * NB), bf16),
             pltpu.VMEM((NB * 6, 6 * NB), f32),
             pltpu.VMEM((3, rows, wide), bf16),
-            pltpu.VMEM((slots, 2, ROWS, 3 * wide // 2), f32),
-            pltpu.VMEM((slots, ROWS, 3 * wide // 2), f32),
+            pltpu.VMEM((slots, 2, 3, ROWS, wide // 2), f32),
+            pltpu.VMEM((slots, 3, ROWS, wide // 2), f32),
             pltpu.VMEM((slots, n, ROWS, 3 * pw), bf16),
             pltpu.VMEM((NB, ROWS, 3 * pw), bf16),
             pltpu.VMEM((3, NB * ROWS, pw), f32),
             pltpu.VMEM((NF, 6 * NB, pw), bf16),
             pltpu.VMEM((NF, NB // 2, 4 * NB), f32),
             pltpu.VMEM((total, NB // 2, 4 * NB), f32),
-            pltpu.VMEM((NB + 16, 4 * NB), bf16),
-            pltpu.VMEM((NF, NB + 16, 4 * NB), bf16),
-            dma((5,)), dma((slots,)), dma((slots,)), dma((slots, n)), dma((NB,)),
+            pltpu.VMEM((32, 4 * NB), bf16),
+            pltpu.VMEM((NF, 32, 4 * NB), bf16),
+            dma((5,)), dma((slots, 3)), dma((slots, 3)), dma((slots, n)), dma((NB,)),
             dma((NF,)), dma((total,)), dma((total,)), dma((NF,)),
         ],
         compiler_params=pltpu.CompilerParams(
-            collective_id=0, has_side_effects=True, vmem_limit_bytes=60 * 1024 * 1024),
+            collective_id=0, has_side_effects=True, vmem_limit_bytes=64_500_000),
     )(jnp.transpose(snapshots, (1, 0, 2)), block_starts, freq_index)
     modes = modes.reshape(NF, NB, 3, 2, pw).transpose(0, 1, 3, 2, 4)
-    return modes, energy[:, 0]
+    return modes, energy.reshape(NF)
 
 
 def solution(mesh):

time: 62.9 us -> 63.7 us (1.013)
  Pallas kernels: 58.1 us -> 59.2 us
    slice x1 -> x0, local copies, waits for them, and re-layouts: 1.32 us -> none  [fused(): return (modes, energy[:, 0])]
    pallas_call x1, Pallas kernels: 58.1 us -> 59.2 us  [fused(): pl.pallas_call(functools.partial(kernel, n, nf_dev, per, whole, shared, h...]
    unnamed x1 -> x2, local copies, waits for them, and re-layouts: 2.59 us -> 3.68 us
where the time goes in v4:
time: 63.7 us; the launch traced here: 63.6 us
  Pallas kernels  59.2 us (93%)
  local copies, waits for them, and re-layouts  3.68 us (6%)
  between operations  0.64 us (1%)
    pallas_call x1, Pallas kernels, fused(): pl.pallas_call(functools.partial(kernel, n, nf_dev, per, whole, shared, h...  59.2 us
    unnamed x2, local copies, waits for them, and re-layouts  3.68 us

profile of v4, /device:TPU:0, one launch (start us, length us, event | category | flops | bytes accessed | tf_op | source)
XLA Modules:
  0.0 63.6 jit_solution(3102723378388824620)
XLA Ops:
  0.6 59.2 %shard_map.50 = (bf16[3072,128]{1,0:T(8,128)(2,1)}, f32[1,16]{1,0:T(1,128)}) custom-call(bf16[3,544,1024]{2,1,0:T(8,128)(2,1)} %bitcast.5, s32[32]{0:T(128)} %starts_hbm.1, s32[16]{0:T(128)} %freq_hbm.1), custom_call_target="tpu_custom_call" | custom-call | tf_op jit(solution)/shard_map/pallas_call | solution.py:485
  59.9 2.6 %copy.7 = bf16[16,32,2,3,128]{4,2,3,1,0:T(2,128)(2,1)} copy(bf16[16,32,2,3,128]{4,2,3,1,0:T(2,128)(2,1)} %bitcast.6) | data formatting | bytes 1572864
  62.5 1.1 %copy.8 = f32[16]{0:T(128)} copy(f32[16]{0:T(128)} %bitcast.7) | data formatting | bytes 128

commit v5 on v4

--- a/solution.py
+++ b/solution.py
@@ -234,27 +234,25 @@
     expanders(spread_ref, mask_ref)
     width = xv.shape[2]
     pw = width // n
-    def exchange(slot, c):
+    def exchange(slot):
         low = slot < slots // 2
         there = slot + per if low else slot - per
         return pltpu.make_async_remote_copy(
-            src_ref=parts.at[slot, 1 - parity, c], dst_ref=others.at[there, c],
-            send_sem=psend.at[slot, c], recv_sem=precv.at[there, c],
+            src_ref=parts.at[slot, 1 - parity], dst_ref=others.at[there],
+            send_sem=psend.at[slot], recv_sem=precv.at[there],
             device_id={"tm": (tm + n - 1) % n if low else (tm + 1) % n, "freq": fr},
             device_id_type=MESH)
 
-    def arrival(slot, c):
+    def arrival(slot):
         return pltpu.make_async_remote_copy(
-            src_ref=parts.at[slot, 1 - parity, c], dst_ref=others.at[slot, c],
-            send_sem=psend.at[slot, c], recv_sem=precv.at[slot, c],
+            src_ref=parts.at[slot, 1 - parity], dst_ref=others.at[slot],
+            send_sem=psend.at[slot], recv_sem=precv.at[slot],
             device_id={"tm": tm, "freq": fr}, device_id_type=MESH)
 
     outward = []
     for reach in range(slots // 2):
         outward += [slots // 2 + reach, slots // 2 - 1 - reach]
     inward = [slot + per if slot < slots // 2 else slot - per for slot in outward]
-
-    pl.semaphore_wait(barrier, total - 1)
 
     for c in range(3):
         pltpu.make_async_copy(x_hbm.at[c], xv.at[c], load_sem.at[c]).wait()
@@ -264,11 +262,13 @@
                 at = dest // 2 * pw
                 parts[slot, dest % 2, c, :, at : at + pw] = part[
                     slot * ROWS : (slot + 1) * ROWS, dest * pw : (dest + 1) * pw]
-        for slot in outward:
-            if shared[slot]:
-                @pl.when(member(tm, shared[slot]))
-                def _(slot=slot, c=c):
-                    exchange(slot, c).start()
+    pl.semaphore_wait(barrier, total - 1)
+
+    for slot in outward:
+        if shared[slot]:
+            @pl.when(member(tm, shared[slot]))
+            def _(slot=slot):
+                exchange(slot).start()
 
     def scatter(slot, dest):
         return pltpu.make_async_remote_copy(
@@ -315,8 +315,7 @@
         if shared[slot]:
             @pl.when(member(tm, shared[slot]))
             def _(slot=slot):
-                for c in range(3):
-                    arrival(slot, c).wait_recv()
+                arrival(slot).wait_recv()
                 finish(slot, parity, True)
 
                 @pl.loop(1, half_n)
@@ -418,8 +417,7 @@
         if shared[slot]:
             @pl.when(member(tm, shared[slot]))
             def _(slot=slot):
-                for c in range(3):
-                    exchange(slot, c).wait_send()
+                exchange(slot).wait_send()
 
                 @pl.loop(1, half_n)
                 def _(k):
@@ -504,11 +502,11 @@
             pltpu.VMEM((total, NB // 2, 4 * NB), f32),
             pltpu.VMEM((32, 4 * NB), bf16),
             pltpu.VMEM((NF, 32, 4 * NB), bf16),
-            dma((5,)), dma((slots, 3)), dma((slots, 3)), dma((slots, n)), dma((NB,)),
+            dma((5,)), dma((slots,)), dma((slots,)), dma((slots, n)), dma((NB,)),
             dma((NF,)), dma((total,)), dma((total,)), dma((NF,)),
         ],
         compiler_params=pltpu.CompilerParams(
-            collective_id=0, has_side_effects=True, vmem_limit_bytes=64_500_000),
+            collective_id=0, has_side_effects=True, vmem_limit_bytes=54_000_000),
     )(jnp.transpose(snapshots, (1, 0, 2)), block_starts, freq_index)
     modes = modes.reshape(NF, NB, 3, 2, pw).transpose(0, 1, 3, 2, 4)
     return modes, energy.reshape(NF)

time: 63.7 us -> 59 us (0.926)
  Pallas kernels: 59.2 us -> 55.5 us
  local copies, waits for them, and re-layouts: 3.68 us -> 2.7 us
    pallas_call x1, Pallas kernels: 59.2 us -> 55.5 us  [fused(): pl.pallas_call(functools.partial(kernel, n, nf_dev, per, whole, shared, h...]
    unnamed x2 -> x6, local copies, waits for them, and re-layouts: 3.68 us -> 2.7 us
where the time goes in v5:
time: 59 us; the launch traced here: 58.9 us
  Pallas kernels  55.5 us (94%)
  local copies, waits for them, and re-layouts  2.7 us (5%)
  between operations  0.65 us (1%)
    pallas_call x1, Pallas kernels, fused(): pl.pallas_call(functools.partial(kernel, n, nf_dev, per, whole, shared, h...  55.5 us
    unnamed x6, local copies, waits for them, and re-layouts  2.7 us

profile of v5, /device:TPU:0, one launch (start us, length us, event | category | flops | bytes accessed | tf_op | source)
XLA Modules:
  0.0 58.9 jit_solution(7331724187440838712)
XLA Ops:
  0.6 0.0 copy-start
  0.6 0.6 %copy-done = s32[32]{0:T(128)S(1)} copy-done((s32[32]{0:T(128)S(1)}, s32[32]{0:T(128)}, u32[]{:S(2)}) %copy-start) | copy-done | bytes 152
  1.3 0.0 copy-start.1
  1.3 0.7 %copy-done.1 = s32[16]{0:T(128)S(1)} copy-done((s32[16]{0:T(128)S(1)}, s32[16]{0:T(128)}, u32[]{:S(2)}) %copy-start.1) | copy-done | bytes 88
  1.9 55.5 %shard_map.50 = (bf16[3072,128]{1,0:T(8,128)(2,1)S(1)}, f32[1,16]{1,0:T(1,128)S(1)}) custom-call(bf16[3,544,1024]{2,1,0:T(8,128)(2,1)} %bitcast.7, s32[32]{0:T(128)S(1)} %copy-done, s32[16]{0:T(128)S(1)} %copy-done.1), custom_call_target="tpu_custom_call" | custom-call | tf_op jit(solution)/shard_map/pallas_call | solution.py:483
  57.5 0.9 %copy.7 = bf16[16,32,2,3,128]{4,2,3,1,0:T(2,128)(2,1)} copy(bf16[16,32,2,3,128]{4,2,3,1,0:T(2,128)(2,1)S(1)} %bitcast.5) | data formatting | bytes 1572864
  58.4 0.5 copy.8
Async XLA Ops:
  0.6 0.7 %copy-start = (s32[32]{0:T(128)S(1)}, s32[32]{0:T(128)}, u32[]{:S(2)}) copy-start(s32[32]{0:T(128)} %starts_hbm.1) | copy-start | bytes 388
  1.3 0.7 %copy-start.1 = (s32[16]{0:T(128)S(1)}, s32[16]{0:T(128)}, u32[]{:S(2)}) copy-start(s32[16]{0:T(128)} %freq_hbm.1) | copy-start | bytes 196

commit v6 on v5

--- a/solution.py
+++ b/solution.py
@@ -138,12 +138,12 @@
     return per, whole, shared, holders
 
 
-def base_table(freq_ref):
+def base_table(ints_ref):
     row = lax.broadcasted_iota(jnp.int32, (ROWS, NFFT), 0)
     times_idx = lax.broadcasted_iota(jnp.int32, (ROWS, NFFT), 1)
     freqs = jnp.zeros((ROWS, NFFT), jnp.int32)
     for f in range(NF):
-        freqs = jnp.where((row >> 1) == f, freq_ref[f], freqs)
+        freqs = jnp.where((row >> 1) == f, ints_ref[NB + f], freqs)
     phase = (freqs * times_idx) & (NFFT - 1)
     angles = 2.0 * math.pi / NFFT * phase.astype(jnp.float32)
     window = 0.5 - 0.5 * jnp.cos(2.0 * math.pi / NFFT * times_idx.astype(jnp.float32))
@@ -186,8 +186,8 @@
     return hit
 
 
-def kernel(n, nf_dev, per, whole, shared, holders, points, x_hbm, starts_hbm, freq_hbm,
-           modes_ref, energy_ref, starts_ref, freq_ref, t_ref, spread_ref, mask_ref, xv, parts,
+def kernel(n, nf_dev, per, whole, shared, holders, points, x_hbm, ints_hbm,
+           modes_ref, energy_ref, ints_ref, t_ref, spread_ref, mask_ref, xv, parts,
            others, sendb, recvb, spec32, spec, gpart, gath, msg, crecv, load_sem, psend, precv,
            asend, arecv, gsend, grecv, csend, crcv):
     tm = lax.axis_index("tm")
@@ -207,12 +207,8 @@
     def where_is(index):
         return {"tm": index // nf_dev, "freq": index % nf_dev}
 
-    small = [
-        pltpu.make_async_copy(starts_hbm, starts_ref, load_sem.at[3]),
-        pltpu.make_async_copy(freq_hbm, freq_ref, load_sem.at[4]),
-    ]
-    for copy in small:
-        copy.start()
+    small = pltpu.make_async_copy(ints_hbm, ints_ref, load_sem.at[3])
+    small.start()
     for c in range(3):
         pltpu.make_async_copy(x_hbm.at[c], xv.at[c], load_sem.at[c]).start()
     barrier = pltpu.get_barrier_semaphore()
@@ -221,13 +217,12 @@
     def _(k):
         pl.semaphore_signal(barrier, inc=1, device_id=where_is((lin + k) % total), device_id_type=MESH)
 
-    for copy in small:
-        copy.wait()
+    small.wait()
     rows = xv.shape[1]
-    base = base_table(freq_ref)
+    base = base_table(ints_ref)
     for slot in range(slots):
         block = per * tm + slot - 2
-        start = starts_ref[jnp.clip(block, 0, NB - 1)]
+        start = ints_ref[jnp.clip(block, 0, NB - 1)]
         inside = (block >= 0) & (block < NB)
         shift = jnp.where(inside, rows * tm - start, 4 * (rows + NFFT))
         t_ref[slot * ROWS : (slot + 1) * ROWS, :] = shifted(base, shift, rows)
@@ -254,21 +249,31 @@
         outward += [slots // 2 + reach, slots // 2 - 1 - reach]
     inward = [slot + per if slot < slots // 2 else slot - per for slot in outward]
 
+    def compute(first, last):
+        for c in range(3):
+            part = jnp.dot(t_ref[first * ROWS : last * ROWS, :], xv[c], preferred_element_type=jnp.float32)
+            for slot in range(first, last):
+                for dest in range(n):
+                    at = dest // 2 * pw
+                    parts[slot, dest % 2, c, :, at : at + pw] = part[
+                        (slot - first) * ROWS : (slot - first + 1) * ROWS, dest * pw : (dest + 1) * pw]
+
+    def send_parts(chosen):
+        for slot in chosen:
+            if shared[slot]:
+                @pl.when(member(tm, shared[slot]))
+                def _(slot=slot):
+                    exchange(slot).start()
+
     for c in range(3):
         pltpu.make_async_copy(x_hbm.at[c], xv.at[c], load_sem.at[c]).wait()
-        part = jnp.dot(t_ref[...], xv[c], preferred_element_type=jnp.float32)
-        for slot in range(slots):
-            for dest in range(n):
-                at = dest // 2 * pw
-                parts[slot, dest % 2, c, :, at : at + pw] = part[
-                    slot * ROWS : (slot + 1) * ROWS, dest * pw : (dest + 1) * pw]
+    inner = [slot for slot in outward if 2 <= slot < slots - 2]
+    compute(2, slots - 2)
     pl.semaphore_wait(barrier, total - 1)
-
-    for slot in outward:
-        if shared[slot]:
-            @pl.when(member(tm, shared[slot]))
-            def _(slot=slot):
-                exchange(slot).start()
+    send_parts(inner)
+    compute(0, 2)
+    compute(slots - 2, slots)
+    send_parts([slot for slot in outward if slot not in inner])
 
     def scatter(slot, dest):
         return pltpu.make_async_remote_copy(
@@ -483,11 +488,10 @@
     modes, energy = pl.pallas_call(
         functools.partial(kernel, n, nf_dev, per, whole, shared, holders, float(wide * nf_dev)),
         out_shape=(jax.ShapeDtypeStruct((NF * NB * 6, pw), bf16), jax.ShapeDtypeStruct((1, NF), f32)),
-        in_specs=[pl.BlockSpec(memory_space=pltpu.HBM)] * 3,
+        in_specs=[pl.BlockSpec(memory_space=pltpu.HBM)] * 2,
         out_specs=(vmem, vmem),
         scratch_shapes=[
-            pltpu.SMEM((NB,), jnp.int32),
-            pltpu.SMEM((NF,), jnp.int32),
+            pltpu.SMEM((NB + NF,), jnp.int32),
             pltpu.VMEM((slots * ROWS, rows), bf16),
             pltpu.VMEM((NB * 6, 2 * NB), bf16),
             pltpu.VMEM((NB * 6, 6 * NB), f32),
@@ -502,12 +506,12 @@
             pltpu.VMEM((total, NB // 2, 4 * NB), f32),
             pltpu.VMEM((32, 4 * NB), bf16),
             pltpu.VMEM((NF, 32, 4 * NB), bf16),
-            dma((5,)), dma((slots,)), dma((slots,)), dma((slots, n)), dma((NB,)),
+            dma((4,)), dma((slots,)), dma((slots,)), dma((slots, n)), dma((NB,)),
             dma((NF,)), dma((total,)), dma((total,)), dma((NF,)),
         ],
         compiler_params=pltpu.CompilerParams(
             collective_id=0, has_side_effects=True, vmem_limit_bytes=54_000_000),
-    )(jnp.transpose(snapshots, (1, 0, 2)), block_starts, freq_index)
+    )(jnp.transpose(snapshots, (1, 0, 2)), jnp.concatenate([block_starts, freq_index]))
     modes = modes.reshape(NF, NB, 3, 2, pw).transpose(0, 1, 3, 2, 4)
     return modes, energy.reshape(NF)
 

time: 59 us -> 58.2 us (0.986)
  local copies, waits for them, and re-layouts: 2.7 us -> 1.39 us
  other arithmetic: 0 us -> 0.75 us
    unnamed x6 -> x2, local copies, waits for them, and re-layouts: 2.7 us -> 1.39 us
    concatenate x0 -> x1, other arithmetic: none -> 0.75 us  [fused(): jnp.concatenate([block_starts, freq_index])]
where the time goes in v6:
time: 58.2 us; the launch traced here: 58.1 us
  Pallas kernels  55.3 us (95%)
  local copies, waits for them, and re-layouts  1.39 us (2%)
  other arithmetic  0.75 us (1%)
  between operations  0.64 us (1%)
    pallas_call x1, Pallas kernels, fused(): pl.pallas_call(functools.partial(kernel, n, nf_dev, per, whole, shared, h...  55.3 us
    unnamed x2, local copies, waits for them, and re-layouts  1.39 us

profile of v6, /device:TPU:0, one launch (start us, length us, event | category | flops | bytes accessed | tf_op | source)
XLA Modules:
  0.0 58.1 jit_solution(3537304485672514483)
XLA Ops:
  0.6 0.7 %pad_add_fusion.ints_hbm = s32[48]{0:T(128)S(1)} fusion(s32[16]{0:T(128)} %param.5, s32[32]{0:T(128)} %param.4), kind=kLoop, calls=%fused_computation | loop fusion | flops 48 | bytes 384 | tf_op jit(solution)/shard_map/concatenate | solution.py:514
  1.4 55.3 %shard_map.50 = (bf16[3072,128]{1,0:T(8,128)(2,1)S(1)}, f32[1,16]{1,0:T(1,128)S(1)}) custom-call(bf16[3,544,1024]{2,1,0:T(8,128)(2,1)} %bitcast.7, s32[48]{0:T(128)S(1)} %pad_add_fusion.ints_hbm), custom_call_target="tpu_custom_call" | custom-call | tf_op jit(solution)/shard_map/pallas_call | solution.py:488
  56.7 0.9 %copy.7 = bf16[16,32,2,3,128]{4,2,3,1,0:T(2,128)(2,1)} copy(bf16[16,32,2,3,128]{4,2,3,1,0:T(2,128)(2,1)S(1)} %bitcast.5) | data formatting | bytes 1572864
  57.6 0.5 copy.8
